TPU v7x, 8 devices: a whole 2x2x1 slice. The times are simulated.
8 devices in a mesh: dp: 1 (over z), dm: 2 (over y), tp: 4 (over x, core).
Axes of the slice: x: 2, y: 2, z: 1, core: 2. Of those that a mesh axis runs over, the one named last changes fastest.
Arguments:
- hidden: bfloat16 [128, 8192], P('dp', 'dm')
- w_q: bfloat16 [8192, 64, 128], P('dm', 'tp')
- w_k: bfloat16 [8192, 8, 128], P('dm', 'tp')
- w_v: bfloat16 [8192, 8, 128], P('dm', 'tp')
- w_o: bfloat16 [64, 128, 8192], P('tp', None, 'dm')
- w_gate: bfloat16 [8192, 22016], P('dm', 'tp')
- w_up: bfloat16 [8192, 22016], P('dm', 'tp')
- w_down: bfloat16 [22016, 8192], P('tp', 'dm')
- norm_attn: bfloat16 [8192], P('dm')
- norm_mlp: bfloat16 [8192], P('dm')
- k_cache: bfloat16 [128, 128, 8, 128], P(('dp', 'dm'), None, 'tp')
- v_cache: bfloat16 [128, 128, 8, 128], P(('dp', 'dm'), None, 'tp')
- seq_lens: int32 [128], P(('dp', 'dm'))
- rope_cos: float32 [128, 64], P(('dp', 'dm'))
- rope_sin: float32 [128, 64], P(('dp', 'dm'))
Outputs:
- output 1: bfloat16 [128, 8192], P('dp', 'dm')
- output 2: bfloat16 [128, 128, 8, 128], P(('dp', 'dm'), None, 'tp')
- output 3: bfloat16 [128, 128, 8, 128], P(('dp', 'dm'), None, 'tp')
All inputs are finite; a program needn't handle non-finite values.
Results may differ from a plain program's by a relative error of at most 0.0105769.
Values are sent between devices in bfloat16 or wider.
A program may use at most 1 GiB of HBM per device.

v0:
```python
import jax
import jax.numpy as jnp
from jax import lax
from jax.sharding import PartitionSpec as P

EPS = 1e-6


def width_norm(x, gain, width_full):
    x_f32 = x.astype(jnp.float32)
    sq_sum = lax.psum(jnp.sum(x_f32 * x_f32, axis=-1, keepdims=True), 'dm')
    scale = lax.rsqrt(sq_sum / width_full + EPS)
    return (x_f32 * scale * gain.astype(jnp.float32)).astype(jnp.bfloat16)


def apply_rope(x, rope_cos, rope_sin):
    half = x.shape[-1] // 2
    first = x[..., :half]
    second = x[..., half:]
    cosine = rope_cos[:, None, :]
    sine = rope_sin[:, None, :]
    return jnp.concatenate([first * cosine - second * sine, second * cosine + first * sine], axis=-1).astype(jnp.bfloat16)


def attend(q_rot, k_rot, v_new, k_cache, v_cache, seq_lens):
    rows, seq_len, kv_local, head_dim = k_cache.shape
    positions = jnp.arange(seq_len)
    write_mask = (positions[None, :] == seq_lens[:, None])[:, :, None, None]
    k_out = jnp.where(write_mask, k_rot[:, None], k_cache)
    v_out = jnp.where(write_mask, v_new[:, None], v_cache)
    q_grp = q_rot.reshape(rows, kv_local, -1, head_dim)
    scores = jnp.einsum('bkgd,bskd->bkgs', q_grp, k_out, preferred_element_type=jnp.float32) * (head_dim ** -0.5)
    key_mask = (positions[None, :] <= seq_lens[:, None])[:, None, None, :]
    scores = jnp.where(key_mask, scores, -1e30)
    attn_probs = jax.nn.softmax(scores, axis=-1).astype(jnp.bfloat16)
    heads = jnp.einsum('bkgs,bskd->bkgd', attn_probs, v_out, preferred_element_type=jnp.float32)
    return heads.astype(jnp.bfloat16).reshape(rows, -1, head_dim), k_out, v_out


def solution(mesh):
    width_shards = mesh.shape['dm']
    row_spec = P('dp', 'dm')
    cache_spec = P(('dp', 'dm'), None, 'tp', None)
    batch_spec = P(('dp', 'dm'))
    rope_spec = P(('dp', 'dm'), None)
    in_specs = (row_spec, P('dm', 'tp', None), P('dm', 'tp', None), P('dm', 'tp', None), P('tp', None, 'dm'), P('dm', 'tp'), P('dm', 'tp'), P('tp', 'dm'), P('dm'), P('dm'), cache_spec, cache_spec, batch_spec, rope_spec, rope_spec)
    out_specs = (row_spec, cache_spec, cache_spec)

    def local_layer(hidden, w_q, w_k, w_v, w_o, w_gate, w_up, w_down, norm_attn, norm_mlp, k_cache, v_cache, seq_lens, rope_cos, rope_sin):
        width_full = hidden.shape[1] * width_shards
        x_norm = width_norm(hidden, norm_attn, width_full)
        q_part = jnp.einsum('bd,dhk->bhk', x_norm, w_q, preferred_element_type=jnp.float32)
        k_part = jnp.einsum('bd,dhk->bhk', x_norm, w_k, preferred_element_type=jnp.float32)
        v_part = jnp.einsum('bd,dhk->bhk', x_norm, w_v, preferred_element_type=jnp.float32)
        q_rows = lax.psum_scatter(q_part, 'dm', scatter_dimension=0, tiled=True)
        k_rows = lax.psum_scatter(k_part, 'dm', scatter_dimension=0, tiled=True)
        v_rows = lax.psum_scatter(v_part, 'dm', scatter_dimension=0, tiled=True)
        q_rot = apply_rope(q_rows, rope_cos, rope_sin)
        k_rot = apply_rope(k_rows, rope_cos, rope_sin)
        attn_heads, k_out, v_out = attend(q_rot, k_rot, v_rows.astype(jnp.bfloat16), k_cache, v_cache, seq_lens)
        heads_all = lax.all_gather(attn_heads, 'dm', axis=0, tiled=True)
        attn_part = jnp.einsum('bhk,hkd->bd', heads_all, w_o, preferred_element_type=jnp.float32)
        attn_out = lax.psum(attn_part, 'tp').astype(jnp.bfloat16)
        h_mid = hidden + attn_out
        x_mlp = width_norm(h_mid, norm_mlp, width_full)
        gate = lax.psum(jnp.dot(x_mlp, w_gate, preferred_element_type=jnp.float32), 'dm')
        up_proj = lax.psum(jnp.dot(x_mlp, w_up, preferred_element_type=jnp.float32), 'dm')
        gated_act = (jax.nn.silu(gate) * up_proj).astype(jnp.bfloat16)
        mlp_out = lax.psum(jnp.dot(gated_act, w_down, preferred_element_type=jnp.float32), 'tp').astype(jnp.bfloat16)
        return h_mid + mlp_out, k_out, v_out

    return jax.shard_map(local_layer, mesh=mesh, in_specs=in_specs, out_specs=out_specs, check_vma=False)
```

profile of v0, /device:TPU:0, one launch (start us, length us, event | category | flops | bytes accessed | tf_op | source)
XLA Modules:
  0.0 374.0 jit_solution(4426286400782009308)
XLA Ops:
  7.2 0.0 copy-start
  7.2 0.0 copy-start.2
  7.2 0.0 reduce-scatter.6.cloned.1.call-start
  7.2 1.7 fusion.7
  8.9 6.3 %psum.42 = f32[128,1]{0,1:T(1,128)S(1)} all-reduce(f32[128,1]{0,1:T(1,128)S(1)} %bitcast.24), channel_id=1, replica_groups=mesh['dp'=1,'dm'=2,'tp'=4] {'dm'}, use_global_device_ids=true, to_apply=%region_1.0 | all-reduce | flops 128 | bytes 1024 | tf_op jit(solution)/shard_map/psum | solution.py:11
  15.2 0.7 convert_element_type.44
  15.9 0.0 copy-done
  15.9 2.5 fusion.15
  18.4 0.0 reduce-scatter.6.cloned.1.call-update
  18.4 0.0 reduce-scatter.8.cloned.1.call-start
  18.4 0.0 copy-done.2
  18.5 2.9 fusion.13
  21.3 0.0 reduce-scatter.8.cloned.1.call-update
  21.3 0.0 copy-start.5
  21.3 0.0 copy-start.6
  21.4 0.0 copy-start.3
  21.4 0.0 copy-start.4
  21.4 0.0 reduce-scatter.4.cloned.1.call-start
  21.4 9.6 %fusion.1 = f32[128,16,128]{2,0,1:T(8,128)} fusion(bf16[4096,16,128]{2,1,0:T(8,128)(2,1)} %param.16, bf16[128,4096]{1,0:T(8,128)(2,1)S(1)} %copy-done.2, f32[4096]{0:T(1024)S(1)} %convert_element_type.44, f32[128]{0:T(128)S(1)} %rsqrt_bitcast_fusion.1), kind=kOutput, calls=%fused_computation.1 | convolution fusion | flops 2149580800 | bytes 18891264 | tf_op jit(solution)/shard_map/bd,dhk->bhk/dot_general | solution.py:52
  31.0 0.0 reduce-scatter.4.cloned.1.call-update
  31.0 0.0 all-reduce.5.cloned.1.call-start
  31.1 0.0 copy-done.5
  31.1 0.0 copy-done.6
  31.1 0.1 iota_compare_fusion.1
  31.2 0.0 reduce-scatter.6.cloned.1.call-done
  31.2 0.0 copy-done.3
  31.2 0.0 copy-done.4
  31.2 1.0 subtract_convert_fusion.1
  32.2 0.1 pad_maximum_fusion
  32.4 5.6 %reduce-scatter.8.cloned.1.call-done = f32[64,2,128]{2,0,1:T(8,128)} async-done(((f32[128,2,128]{2,0,1:T(8,128)}), f32[64,2,128]{2,0,1:T(8,128)}) %reduce-scatter.8.cloned.1.call-update) | async-done | bytes 65552 | tf_op jit(solution)/shard_map/reduce_scatter | solution.py:57
  37.9 0.8 convert_element_type.47
  38.8 13.8 %broadcast_select_fusion.1 = (bf16[64,128,2,128]{3,2,1,0:T(2,128)(2,1)}, bf16[64,128,2,128]{3,2,1,0:T(2,128)(2,1)}) fusion(bf16[64,128,2,128]{3,2,1,0:T(2,128)(2,1)} %param.25, pred[64,128]{1,0:T(8,128)(4,1)S(1)} %get-tuple-element.14, bf16[64,2,128]{2,1,0:T(2,128)(2,1)S(1)} %copy.22, bf16[64,128,2,128]{3,2,1,0:T(2,128)(2,1)} %param.26, ...), kind=kLoop, calls=%fused_computation.4 | loop fusion | flops 4194304 | bytes 16850944 | tf_op jit(solution)/shard_map/jit(_where)/select_n | solution.py:29
  52.6 5.7 %reduce-scatter.4.cloned.1.call-done = f32[64,16,128]{2,0,1:T(8,128)} async-done(((f32[128,16,128]{2,0,1:T(8,128)}), f32[64,16,128]{2,0,1:T(8,128)}) %reduce-scatter.4.cloned.1.call-update) | async-done | bytes 524304 | tf_op jit(solution)/shard_map/reduce_scatter | solution.py:55
  58.3 1.4 subtract_convert_fusion
  59.7 0.2 copy.19
  59.9 0.2 copy.20
  60.1 4.7 %fusion.47 = (f32[64,2,8]{2,1,0:T(2,128)S(1)}, f32[64,2,8,128]{3,2,1,0:T(8,128)S(1)}) fusion(bf16[64,128,2,128]{3,2,1,0:T(2,128)(2,1)} %get-tuple-element.11, bf16[64,2,8,64]{3,2,1,0:T(8,128)(2,1)S(1)} %copy.20, bf16[64,2,8,64]{3,2,1,0:T(8,128)(2,1)S(1)} %copy.19, pred[64,128]{1,0:T(8,128)(4,1)S(1)} %get-tuple-element.13), kind=kOutput, calls=%fused_computation.54 | convolution fusion | flops 34603136 | bytes 4993024 | tf_op jit(solution)/shard_map/sub | solution.py:35
  64.8 3.4 fusion.30
  68.2 0.1 copy.27
  68.3 8.5 %all_gather.3 = bf16[128,16,128]{2,0,1:T(8,128)(2,1)S(1)} all-gather(bf16[64,16,128]{2,0,1:T(8,128)(2,1)S(1)} %copy.27), channel_id=1, replica_groups=mesh['dp'=1,'dm'=2,'tp'=4] {'dm'}, dimensions={0}, use_global_device_ids=true | all-gather | bytes 786432 | tf_op jit(solution)/shard_map/all_gather | solution.py:61
  76.8 7.1 %convolution_bitcast_fusion = f32[128,4096]{1,0:T(8,128)S(1)} fusion(bf16[128,16,128]{2,0,1:T(8,128)(2,1)S(1)} %all_gather.3, bf16[16,128,4096]{2,1,0:T(8,128)(2,1)} %param.19), kind=kOutput, calls=%fused_computation.5 | convolution fusion | flops 2147483648 | bytes 19398656 | tf_op jit(solution)/shard_map/bhk,hkd->bd/dot_general | solution.py:62
  83.9 40.5 %all-reduce.6 = bf16[128,4096]{1,0:T(8,128)(2,1)} all-reduce(f32[128,4096]{1,0:T(8,128)S(1)} %convolution_bitcast_fusion), channel_id=1, replica_groups=mesh['dp'=1,'dm'=2,'tp'=4] {'tp'}, use_global_device_ids=true, to_apply=%region_7.8 | all-reduce | flops 524288 | bytes 3145728 | tf_op jit(solution)/shard_map/psum | solution.py:63
  124.4 2.0 fusion.10
  126.4 5.1 %psum.44 = f32[128,1]{0,1:T(1,128)S(1)} all-reduce(f32[128,1]{0,1:T(1,128)S(1)} %bitcast.25), channel_id=1, replica_groups=mesh['dp'=1,'dm'=2,'tp'=4] {'dm'}, use_global_device_ids=true, to_apply=%region_9.10 | all-reduce | flops 128 | bytes 1024 | tf_op jit(solution)/shard_map/psum | solution.py:11
  131.5 18.7 %fusion.34 = f32[128,5504]{1,0:T(8,128)} fusion(bf16[4096,5504]{1,0:T(8,128)(2,1)} %param.21, bf16[128,4096]{1,0:T(8,128)(2,1)S(1)} %get-tuple-element.6, f32[4096]{0:T(1024)S(1)} %convert_element_type.51, f32[128]{0:T(128)S(1)} %rsqrt_bitcast_fusion), kind=kOutput, calls=%fused_computation.39 | convolution fusion | flops 5773459456 | bytes 48972288 | tf_op jit(solution)/shard_map/dot_general | solution.py:67
  150.3 18.7 %fusion.36 = f32[128,5504]{1,0:T(8,128)} fusion(bf16[4096,5504]{1,0:T(8,128)(2,1)} %param.20, bf16[128,4096]{1,0:T(8,128)(2,1)S(1)} %get-tuple-element.6, f32[4096]{0:T(1024)S(1)} %convert_element_type.51, f32[128]{0:T(128)S(1)} %rsqrt_bitcast_fusion), kind=kOutput, calls=%fused_computation.40 | convolution fusion | flops 5773459456 | bytes 48972288 | tf_op jit(solution)/shard_map/dot_general | solution.py:66
  169.0 0.0 all-reduce.5.cloned.1.call-update
  169.0 133.9 %all-reduce.5.cloned.1.call-done = (f32[128,5504]{1,0:T(8,128)}, f32[128,5504]{1,0:T(8,128)}) async-done(((f32[128,5504]{1,0:T(8,128)}, f32[128,5504]{1,0:T(8,128)}), (f32[128,5504]{1,0:T(8,128)}, f32[128,5504]{1,0:T(8,128)})) %all-reduce.5.cloned.1.call-update) | async-done | bytes 5636112 | tf_op jit(solution)/shard_map/psum | solution.py:67
  302.9 0.0 copy-start.1
  302.9 20.3 %fusion.17 = f32[128,4096]{1,0:T(8,128)} fusion(bf16[5504,4096]{1,0:T(8,128)(2,1)} %param.22, f32[128,5504]{1,0:T(8,128)} %get-tuple-element.3, f32[128,5504]{1,0:T(8,128)} %get-tuple-element.4), kind=kOutput, calls=%fused_computation.25 | convolution fusion | flops 5775589376 | bytes 52822016 | tf_op jit(solution)/shard_map/dot_general | solution.py:69
  323.2 41.8 %all-reduce.7 = bf16[128,4096]{1,0:T(8,128)(2,1)} all-reduce(f32[128,4096]{1,0:T(8,128)} %fusion.17), channel_id=1, replica_groups=mesh['dp'=1,'dm'=2,'tp'=4] {'tp'}, use_global_device_ids=true, to_apply=%region_12.13 | all-reduce | flops 524288 | bytes 3145728 | tf_op jit(solution)/shard_map/psum | solution.py:69
  365.1 2.4 add.55
  367.5 0.0 copy-done.1
  (5 shorter events, 0.1 us)
Async XLA Ops:
  7.2 8.7 %copy-start = (bf16[4096,2,128]{2,1,0:T(2,128)(2,1)S(1)}, bf16[4096,2,128]{2,1,0:T(2,128)(2,1)}, u32[]{:S(2)}) copy-start(bf16[4096,2,128]{2,1,0:T(2,128)(2,1)} %param.17) | copy-start | bytes 6291460
  7.2 11.3 %copy-start.2 = (bf16[128,4096]{1,0:T(8,128)(2,1)S(1)}, bf16[128,4096]{1,0:T(8,128)(2,1)}, u32[]{:S(2)}) copy-start(bf16[128,4096]{1,0:T(8,128)(2,1)} %param.15) | copy-start | bytes 3145732
  7.2 24.0 %reduce-scatter.6.cloned.1.call-start = ((), (), s32[]{:S(2)}) async-start(), calls=%async_computation.4 | async-start | bytes 196608 | tf_op jit(solution)/shard_map/reduce_scatter | solution.py:56
  18.4 19.5 %reduce-scatter.8.cloned.1.call-start = ((), (), s32[]{:S(2)}) async-start(), calls=%async_computation.5 | async-start | bytes 196608 | tf_op jit(solution)/shard_map/reduce_scatter | solution.py:57
  21.3 9.7 %copy-start.5 = (bf16[4096]{0:T(1024)(128)(2,1)S(1)}, bf16[4096]{0:T(1024)(128)(2,1)}, u32[]{:S(2)}) copy-start(bf16[4096]{0:T(1024)(128)(2,1)} %param.24) | copy-start | bytes 24580
  21.3 9.7 %copy-start.6 = (s32[64]{0:T(128)S(1)}, s32[64]{0:T(128)}, u32[]{:S(2)}) copy-start(s32[64]{0:T(128)} %param.27) | copy-start | bytes 772
  21.4 9.9 %copy-start.3 = (f32[64,64]{1,0:T(8,128)S(1)}, f32[64,64]{1,0:T(8,128)}, u32[]{:S(2)}) copy-start(f32[64,64]{1,0:T(8,128)} %param.29) | copy-start | bytes 49156
  21.4 9.9 %copy-start.4 = (f32[64,64]{1,0:T(8,128)S(1)}, f32[64,64]{1,0:T(8,128)}, u32[]{:S(2)}) copy-start(f32[64,64]{1,0:T(8,128)} %param.28) | copy-start | bytes 49156
  21.4 36.9 %reduce-scatter.4.cloned.1.call-start = ((), (), s32[]{:S(2)}) async-start(), calls=%async_computation.3 | async-start | bytes 1572864 | tf_op jit(solution)/shard_map/reduce_scatter | solution.py:55
  31.0 271.9 %all-reduce.5.cloned.1.call-start = ((), (), s32[]{:S(2)}) async-start(), calls=%async_computation.6 | async-start | bytes 11272192 | tf_op jit(solution)/shard_map/psum | solution.py:67
  302.9 64.6 %copy-start.1 = (bf16[4096,2,128]{2,1,0:T(2,128)(2,1)S(1)}, bf16[4096,2,128]{2,1,0:T(2,128)(2,1)}, u32[]{:S(2)}) copy-start(bf16[4096,2,128]{2,1,0:T(2,128)(2,1)} %param.17) | copy-start | bytes 6291460
Sparse Core Ops, SparseCore 0:
  18.5 9.0 reduce-scatter.5
  30.3 7.5 reduce-scatter.7
  40.7 17.5 reduce-scatter.3
  169.2 133.7 all-reduce.4
where the time goes:
time: 375 us; the launch traced here: 374 us
  waiting for transfers between devices  145 us (39%)
  blocking collectives  102 us (27%)
  matrix products  88 us (23%)
  other arithmetic  24.1 us (6%)
  between operations  14 us (4%)
    psum x1, waiting for transfers between devices, local_layer(): lax.psum(jnp.dot(x_mlp, w_up, preferred_element_type=jnp.float32), 'dm')  134 us
    psum x1, blocking collectives, local_layer(): lax.psum(jnp.dot(gated_act, w_down, preferred_element_type=jnp.float32),...  41.8 us
    psum x1, blocking collectives, local_layer(): attn_out = lax.psum(attn_part, 'tp').astype(jnp.bfloat16)  40.5 us
    dot_general x1, matrix products, local_layer(): jnp.dot(gated_act, w_down, preferred_element_type=jnp.float32)  20.3 us
    dot_general x1, matrix products, local_layer(): jnp.dot(x_mlp, w_gate, preferred_element_type=jnp.float32)  18.7 us
    dot_general x1, matrix products, local_layer(): jnp.dot(x_mlp, w_up, preferred_element_type=jnp.float32)  18.7 us
    select_n x1, other arithmetic, attend(): k_out = jnp.where(write_mask, k_rot[:, None], k_cache)  13.8 us
    psum x2, blocking collectives, width_norm(): sq_sum = lax.psum(jnp.sum(x_f32 * x_f32, axis=-1, keepdims=True), 'dm')  11.4 us
  transfers between devices with their start and end apart: 4, of which 3 were waited for; matrix products, arithmetic and copies ran while one was open for 8% of the time, Pallas kernels for 0%

commit v1 on v0

v1 whole, which is shorter than its diff:
```python
import functools

import jax
import jax.numpy as jnp
from jax import lax
from jax.experimental import pallas as pl
from jax.experimental.pallas import tpu as pltpu
from jax.sharding import PartitionSpec as P

EPS = 1e-6
MESH = pl.DeviceIdType.MESH
F32 = jnp.float32
BF16 = jnp.bfloat16
ANY = pl.BlockSpec(memory_space=pl.ANY)
VM = pl.BlockSpec(memory_space=pltpu.VMEM)
SM = pl.BlockSpec(memory_space=pltpu.SMEM)


def me():
    return lax.axis_index('dp'), lax.axis_index('dm'), lax.axis_index('tp')


def row_to_lanes(col):
    return jnp.broadcast_to(col, (128, 128)).T[0:8, :]


def lanes_to_row(vec):
    return jnp.broadcast_to(vec, (128, 128)).T[:, 0:1]


def norm_kernel(width_full, h_ref, g_ref, x_ref, mine, theirs, ssem, rsem):
    dp, dm, tp = me()
    peer = (dp, 1 - dm, tp)
    bar = pltpu.get_barrier_semaphore()
    pl.semaphore_signal(bar, inc=1, device_id=peer, device_id_type=MESH)
    h = h_ref[...].astype(F32)
    mine[...] = row_to_lanes(jnp.sum(h * h, axis=-1, keepdims=True))
    pl.semaphore_wait(bar, 1)
    cp = pltpu.make_async_remote_copy(mine, theirs, ssem, rsem, device_id=peer, device_id_type=MESH)
    cp.start()
    cp.wait()
    total = lanes_to_row(mine[0:1, :] + theirs[0:1, :])
    scale = lax.rsqrt(total / width_full + EPS)
    for r in range(4):
        rows = slice(32 * r, 32 * r + 32)
        x_ref[rows, :] = (h_ref[rows, :].astype(F32) * scale[rows, :] * g_ref[...].astype(F32)).astype(BF16)


def norm_call(hidden, gain, width_full):
    return pl.pallas_call(
        functools.partial(norm_kernel, width_full),
        out_shape=jax.ShapeDtypeStruct(hidden.shape, BF16),
        in_specs=[VM, VM], out_specs=VM,
        scratch_shapes=[pltpu.VMEM((8, 128), F32), pltpu.VMEM((8, 128), F32), pltpu.SemaphoreType.DMA, pltpu.SemaphoreType.DMA],
        compiler_params=pltpu.CompilerParams(collective_id=0, has_side_effects=True, vmem_limit_bytes=24 * 2**20),
        name='norm_x',
    )(hidden, gain)


QCH = 8


def rope_kernel(q_ref, kv_ref, cos_ref, sin_ref, qo_ref, kvo_ref, qbuf, kvbuf, ss, rs):
    dp, dm, tp = me()
    peer = (dp, 1 - dm, tp)
    mine = pl.ds(pl.multiple_of(dm * 64, 64), 64)
    other = pl.ds(pl.multiple_of((1 - dm) * 64, 64), 64)
    bar = pltpu.get_barrier_semaphore()
    pl.semaphore_signal(bar, inc=1, device_id=peer, device_id_type=MESH)
    pl.semaphore_wait(bar, 1)
    cps = []
    for i in range(QCH):
        n = 16 // QCH
        cps.append(pltpu.make_async_remote_copy(q_ref.at[i * n:(i + 1) * n, other, :], qbuf.at[i * n:(i + 1) * n], ss.at[i], rs.at[i],
                                                device_id=peer, device_id_type=MESH))
    cps.append(pltpu.make_async_remote_copy(kv_ref.at[:, other, :], kvbuf, ss.at[QCH], rs.at[QCH], device_id=peer, device_id_type=MESH))
    for cp in cps:
        cp.start()
    c = cos_ref[...]
    s = sin_ref[...]
    cos2 = jnp.concatenate([c, c], axis=-1)
    sin2 = jnp.concatenate([-s, s], axis=-1)

    def rope(a):
        return (a * cos2 + pltpu.roll(a, 64, 1) * sin2).astype(BF16)

    for i in range(QCH):
        cps[i].wait_recv()
        for h in range(i * (16 // QCH), (i + 1) * (16 // QCH)):
            qo_ref[h] = rope(q_ref[h, mine, :] + qbuf[h])
    cps[QCH].wait_recv()
    for h in range(2):
        kvo_ref[h] = rope(kv_ref[h, mine, :] + kvbuf[h])
        kvo_ref[2 + h] = (kv_ref[2 + h, mine, :] + kvbuf[2 + h]).astype(BF16)
    for cp in cps:
        cp.wait_send()


def rope_call(q_part, kv_part, cos, sin):
    return pl.pallas_call(
        rope_kernel,
        out_shape=(jax.ShapeDtypeStruct((16, 64, 128), BF16), jax.ShapeDtypeStruct((4, 64, 128), BF16)),
        in_specs=[VM] * 4, out_specs=(VM, VM),
        scratch_shapes=[pltpu.VMEM((16, 64, 128), F32), pltpu.VMEM((4, 64, 128), F32), pltpu.SemaphoreType.DMA((QCH + 1,)), pltpu.SemaphoreType.DMA((QCH + 1,))],
        compiler_params=pltpu.CompilerParams(collective_id=1, has_side_effects=True, vmem_limit_bytes=24 * 2**20),
        name='rs_rope',
    )(q_part, kv_part, cos, sin)


ACH = 4
AROWS = 64 // ACH


def attn_kernel(q_ref, kv_ref, len_ref, kc, vc, ko, vo, o_ref, kb, vb, qs, os, isem, osem):
    def cin(ch, t):
        rows = pl.ds(ch * AROWS, AROWS)
        return pltpu.make_async_copy((kc, vc)[t].at[rows], (kb, vb)[t].at[rows], isem.at[t, ch])

    def cout(ch, t):
        rows = pl.ds(ch * AROWS, AROWS)
        return pltpu.make_async_copy((kb, vb)[t].at[rows], (ko, vo)[t].at[rows], osem.at[t, ch])

    for ch in range(ACH):
        for t in range(2):
            cin(ch, t).start()
    for h in range(16):
        qs[pl.ds(h, 64, stride=16), :] = q_ref[h].astype(F32)
    row16 = lax.broadcasted_iota(jnp.int32, (16, 128), 0)
    col = lax.broadcasted_iota(jnp.int32, (16, 256), 1)
    head = lax.broadcasted_iota(jnp.int32, (16, 256), 0)
    own = lax.rem(col, 2) == head // 8

    @pl.loop(0, ACH)
    def _(ch):
        cin(ch, 0).wait()
        cin(ch, 1).wait()
        kv32 = [kv_ref[j, pl.ds(pl.multiple_of(ch * AROWS, AROWS), AROWS), :].astype(F32) for j in range(4)]
        for i in range(AROWS):
            b = ch * AROWS + i
            ln = len_ref[b]
            t8 = ln // 8
            at = pl.ds(pl.multiple_of(t8 * 16, 16), 16)
            r0 = 2 * (ln - 8 * t8)
            for t, buf in enumerate((kb, vb)):
                old = buf[b, at, :].astype(F32)
                n0 = jnp.broadcast_to(kv32[2 * t][i:i + 1, :], (16, 128))
                n1 = jnp.broadcast_to(kv32[2 * t + 1][i:i + 1, :], (16, 128))
                new = jnp.where(row16 == r0, n0, jnp.where(row16 == r0 + 1, n1, old))
                buf[b, at, :] = new.astype(BF16)
        cout(ch, 0).start()
        cout(ch, 1).start()
        for i in range(AROWS):
            b = ch * AROWS + i
            ln = len_ref[b]
            q = qs[pl.ds(pl.multiple_of(b * 16, 16), 16), :].astype(BF16)
            s = lax.dot_general(q, kb[b], (((1,), (1,)), ((), ())), preferred_element_type=F32) * (128.0 ** -0.5)
            s = jnp.where(own & (col <= 2 * ln + 1), s, -1e30)
            p = jnp.exp(s - jnp.max(s, axis=-1, keepdims=True))
            p = (p / jnp.sum(p, axis=-1, keepdims=True)).astype(BF16)
            os[pl.ds(pl.multiple_of(b * 16, 16), 16), :] = jnp.dot(p, vb[b], preferred_element_type=F32)

    for h in range(16):
        o_ref[:, h * 128:(h + 1) * 128] = os[pl.ds(h, 64, stride=16), :].astype(BF16)
    for ch in range(ACH):
        cout(ch, 0).wait()
        cout(ch, 1).wait()


def attn_call(q_rot, kv_new, seq_lens, k_cache, v_cache):
    cache = jax.ShapeDtypeStruct((64, 256, 128), BF16)
    return pl.pallas_call(
        attn_kernel,
        out_shape=(cache, cache, jax.ShapeDtypeStruct((64, 2048), BF16)),
        in_specs=[VM, VM, SM, ANY, ANY], out_specs=(ANY, ANY, VM),
        scratch_shapes=[pltpu.VMEM((64, 256, 128), BF16), pltpu.VMEM((64, 256, 128), BF16), pltpu.VMEM((1024, 128), F32), pltpu.VMEM((1024, 128), F32),
                        pltpu.SemaphoreType.DMA((2, ACH)), pltpu.SemaphoreType.DMA((2, ACH))],
        compiler_params=pltpu.CompilerParams(vmem_limit_bytes=32 * 2**20),
        name='attend',
    )(q_rot, kv_new, seq_lens, k_cache, v_cache)


C = 256
N = 22
NB = 3
ND = 8
NR = 4
RB = 128 // NR
LAG = 2
DLAG = 4


def mlp_kernel(width_full, o_ref, hid, gain, wo, wg, wu, wd, out,
               wbuf, dbuf, oall, acc, dd, xs, xr, hq, oq, x2, gown, gsnd, grcv, mall, st,
               wsem, dsem, osem, d2d, xx, agc, agx, fwd, stsem, gs, gr, ms, mr):
    dp, dm, tp = me()
    x = tp // 2
    c = lax.rem(tp, 2)
    ypeer = (dp, 1 - dm, tp)
    cpeer = (dp, dm, x * 2 + 1 - c)
    xpeer = (dp, dm, (1 - x) * 2 + c)
    flat = dm * 4 + tp

    def at_flat(k):
        f = lax.rem(flat + k, 8)
        return f, (dp, f // 4, lax.rem(f, 4))

    def rdma(src, dst, s, r, dev):
        return pltpu.make_async_remote_copy(src, dst, s, r, device_id=dev, device_id_type=MESH)

    def half(d):
        return pl.ds(pl.multiple_of(d * 64, 64), 64)

    def col(ch):
        return pl.multiple_of(ch * C - 128, 128)

    def wcopy(ch, t):
        slot = lax.rem(ch, NB)
        return pltpu.make_async_copy((wg, wu)[t].at[:, pl.ds(col(ch), C)], wbuf.at[slot, t], wsem.at[slot, t])

    def wcopy0(t):
        return pltpu.make_async_copy((wg, wu)[t].at[:, 0:128], wbuf.at[0, t, :, 0:128], wsem.at[0, t])

    def ocopy(j):
        return pltpu.make_async_copy(wo.at[j * C:(j + 1) * C], dbuf.at[j], dsem.at[j])

    def dslot(ch):
        return lax.rem(ch, ND)

    def dcopy(ch):
        slot = dslot(ch)
        return pltpu.make_async_copy(wd.at[pl.ds(col(ch), C)], dbuf.at[slot], dsem.at[slot])

    def dcopy0():
        return pltpu.make_async_copy(wd.at[0:128], dbuf.at[0, 0:128], dsem.at[0])

    for j in range(8):
        ocopy(j).start()

    bar = pltpu.get_barrier_semaphore()
    for k in range(1, 8):
        pl.semaphore_signal(bar, inc=1, device_id=at_flat(k)[1], device_id_type=MESH)
    for t in range(2):
        wcopy0(t).start()
    for ch in range(1, NB):
        for t in range(2):
            wcopy(ch, t).start()
    pl.semaphore_wait(bar, 7)
    ocp = rdma(o_ref, oall, osem.at[0], osem.at[1], ypeer)
    ocp.start()

    def blk(r):
        return slice(r * RB, (r + 1) * RB)

    def d2d_cp(u, r):
        return rdma(acc.at[1 - c, :, blk(r), :], dd.at[:, blk(r), :], d2d.at[u, 0, r], d2d.at[u, 1, r], cpeer)

    def x_cp(u, r):
        return rdma(xs.at[blk(r)], xr.at[blk(r)], xx.at[u, 0, r], xx.at[u, 1, r], xpeer)

    def agc_cp(u, r, buf):
        return rdma(buf.at[tp, blk(r)], buf.at[tp, blk(r)], agc.at[u, 0, r], agc.at[u, 1, r], cpeer)

    def agx_cp(u, r, buf):
        return rdma(buf.at[tp, blk(r)], buf.at[tp, blk(r)], agx.at[u, 0, r], agx.at[u, 1, r], xpeer)

    def fwd_cp(u, r, buf):
        q = lax.rem(tp + 2, 4)
        return rdma(buf.at[q, blk(r)], buf.at[q, blk(r)], fwd.at[u, 0, r], fwd.at[u, 1, r], cpeer)

    def chip_sum(u, r):
        d2d_cp(u, r).wait_recv()
        xs[blk(r), :] = acc[c, 1 - x, blk(r), :] + dd[1 - x, blk(r), :]
        x_cp(u, r).start()

    def total(u, r):
        x_cp(u, r).wait_recv()
        return (acc[c, x, blk(r), :] + dd[x, blk(r), :] + xr[blk(r), :]).astype(BF16)

    def gather(u, r, buf):
        agc_cp(u, r, buf).start()
        agx_cp(u, r, buf).start()

    def relay(u, r, buf):
        agx_cp(u, r, buf).wait_recv()
        fwd_cp(u, r, buf).start()

    def settle(u, buf):
        for r in range(NR):
            agc_cp(u, r, buf).wait_recv()
            fwd_cp(u, r, buf).wait_recv()
        for r in range(NR):
            d2d_cp(u, r).wait_send()
            x_cp(u, r).wait_send()
            agc_cp(u, r, buf).wait_send()
            agx_cp(u, r, buf).wait_send()
            fwd_cp(u, r, buf).wait_send()

    for j in range(8):
        ocopy(j).wait()

    def wo_rows(src, part):
        @pl.loop(0, 8)
        def _(n):
            cols = pl.ds(pl.multiple_of(n * 512, 512), 512)
            v = jnp.dot(src[:, 0:C], dbuf[0, :, cols], preferred_element_type=F32)
            for j in range(1, 8):
                v += jnp.dot(src[:, j * C:(j + 1) * C], dbuf[j, :, cols], preferred_element_type=F32)
            q = n // 2
            acc[lax.rem(q, 2), q // 2, part, pl.ds(pl.multiple_of(lax.rem(n, 2) * 512, 512), 512)] = v

    wo_rows(o_ref, slice(0, 64))
    for r in range(NR // 2):
        d2d_cp(0, r).start()
    for r in range(NR // 2):
        chip_sum(0, r)
    ocp.wait_recv()
    wo_rows(oall, slice(64, 128))
    dcopy0().start()
    for ch in range(1, ND):
        dcopy(ch).start()
    for r in range(NR // 2, NR):
        d2d_cp(0, r).start()
    for r in range(NR // 2, NR):
        chip_sum(0, r)
    qcols = pl.ds(pl.multiple_of(tp * 1024, 1024), 1024)
    sq = []
    for r in range(NR):
        att = total(0, r)
        first = r < NR // 2
        off = (r if first else r - NR // 2) * RB
        rows = pl.ds(pl.multiple_of((dm if first else 1 - dm) * 64 + off, RB), RB)
        h1 = (hid[rows, qcols].astype(F32) + att.astype(F32)).astype(BF16)
        hq[tp, blk(r)] = h1
        gather(0, r, hq)
        h32 = h1.astype(F32)
        sq.append(jnp.sum(h32 * h32, axis=-1, keepdims=True))
    st[flat] = row_to_lanes(jnp.concatenate(sq, axis=0))

    def st_cp(k, own):
        f, dev = at_flat(k)
        if own:
            return rdma(st.at[flat], st.at[flat], stsem.at[0, f], stsem.at[1, flat], dev)
        return rdma(st.at[f], st.at[f], stsem.at[0, f], stsem.at[1, f], dev)

    for k in range(1, 8):
        st_cp(k, True).start()
    for r in range(NR):
        relay(0, r, hq)
    for k in range(1, 8):
        st_cp(k, False).wait_recv()
    tot = jnp.zeros((8, 128), F32)
    for f in range(8):
        v = st[f]
        tot += jnp.where(dm == f // 4, v, pltpu.roll(v, 64, 1))
    scale = lax.rsqrt(lanes_to_row(tot[0:1, :]) / width_full + EPS)
    settle(0, hq)
    for k in range(1, 8):
        st_cp(k, True).wait_send()
    ocp.wait_send()
    for q in range(4):
        for r in range(4):
            rows = slice(32 * r, 32 * r + 32)
            cols = slice(1024 * q, 1024 * q + 1024)
            x2[rows, cols] = (hq[q, rows].astype(F32) * scale[rows, :] * gain[0:1, cols].astype(F32)).astype(BF16)

    def zero_acc():
        for a in range(2):
            for b in range(2):
                acc[a, b] = jnp.zeros((128, 1024), F32)

    zero_acc()

    def g_cp(ch, w=C):
        return rdma(gsnd.at[ch, :, :, 0:w], grcv.at[ch, :, :, 0:w], gs.at[ch], gr.at[ch], ypeer)

    def m_cp(ch, w=C):
        return rdma(mall.at[ch, 0:64, 0:w], mall.at[ch, 64:128, 0:w], ms.at[ch], mr.at[ch], ypeer)

    def up_gate(ch, slot, w=C):
        for t in range(2):
            v = jnp.dot(x2[...], wbuf[slot, t, :, 0:w], preferred_element_type=F32)
            gown[ch, t, :, 0:w] = v[0:64]
            gsnd[ch, t, :, 0:w] = v[64:128]
        g_cp(ch, w).start()

    def act(ch, w=C):
        g_cp(ch, w).wait_recv()
        g = gown[ch, 0, :, 0:w] + grcv[ch, 0, :, 0:w]
        u = gown[ch, 1, :, 0:w] + grcv[ch, 1, :, 0:w]
        mall[ch, 0:64, 0:w] = (g * jax.nn.sigmoid(g) * u).astype(BF16)
        m_cp(ch, w).start()

    def down(ch, slot, w=C):
        m_cp(ch, w).wait_recv()
        m = mall[ch, :, 0:w]

        @pl.loop(0, 4)
        def _(q):
            a, b = lax.rem(q, 2), q // 2
            for n in range(2):
                cols = pl.ds(pl.multiple_of(q * 1024 + n * 512, 512), 512)
                acc[a, b, :, n * 512:(n + 1) * 512] += jnp.dot(m, dbuf[slot, 0:w, cols], preferred_element_type=F32)

    for t in range(2):
        wcopy0(t).wait()
    up_gate(0, 0, 128)
    for t in range(2):
        wcopy(NB, t).start()

    @pl.loop(1, N + DLAG)
    def _(it):
        @pl.when(it < N)
        def _():
            for t in range(2):
                wcopy(it, t).wait()
            up_gate(it, lax.rem(it, NB))

            @pl.when(it + NB < N)
            def _():
                for t in range(2):
                    wcopy(it + NB, t).start()

        @pl.when(it == LAG)
        def _():
            act(0, 128)

        @pl.when((it > LAG) & (it < N + LAG))
        def _():
            act(it - LAG)

        @pl.when(it == DLAG)
        def _():
            dcopy0().wait()
            down(0, 0, 128)
            dcopy(ND).start()

        @pl.when(it > DLAG)
        def _():
            ch = it - DLAG
            dcopy(ch).wait()
            down(ch, dslot(ch))

            @pl.when(ch + ND < N)
            def _():
                dcopy(ch + ND).start()

    for r in range(NR):
        d2d_cp(1, r).start()
    for r in range(NR):
        chip_sum(1, r)
    for r in range(NR):
        mlp = total(1, r)
        oq[tp, blk(r)] = (hq[tp, blk(r)].astype(F32) + mlp.astype(F32)).astype(BF16)
        gather(1, r, oq)
    for r in range(NR):
        relay(1, r, oq)
    settle(1, oq)
    g_cp(0, 128).wait_send()
    m_cp(0, 128).wait_send()

    @pl.loop(1, N)
    def _(ch):
        g_cp(ch).wait_send()
        m_cp(ch).wait_send()

    for q in range(4):
        cols = slice(1024 * q, 1024 * q + 1024)
        out[half(dm), cols] = oq[q, 0:64, :]
        out[half(1 - dm), cols] = oq[q, 64:128, :]


def mlp_call(o, hidden, gain, wo, wg, wu, wd, width_full):
    dma = pltpu.SemaphoreType.DMA
    return pl.pallas_call(
        functools.partial(mlp_kernel, width_full),
        out_shape=jax.ShapeDtypeStruct((128, 4096), BF16),
        in_specs=[VM, VM, VM, ANY, ANY, ANY, ANY], out_specs=VM,
        scratch_shapes=[
            pltpu.VMEM((NB, 2, 4096, C), BF16),
            pltpu.VMEM((ND, C, 4096), BF16),
            pltpu.VMEM((64, 2048), BF16),
            pltpu.VMEM((2, 2, 128, 1024), F32),
            pltpu.VMEM((2, 128, 1024), F32),
            pltpu.VMEM((128, 1024), F32),
            pltpu.VMEM((128, 1024), F32),
            pltpu.VMEM((4, 128, 1024), BF16),
            pltpu.VMEM((4, 128, 1024), BF16),
            pltpu.VMEM((128, 4096), BF16),
            pltpu.VMEM((N, 2, 64, C), F32),
            pltpu.VMEM((N, 2, 64, C), F32),
            pltpu.VMEM((N, 2, 64, C), F32),
            pltpu.VMEM((N, 128, C), BF16),
            pltpu.VMEM((8, 8, 128), F32),
            dma((NB, 2)), dma((ND,)), dma((2,)),
            dma((2, 2, NR)), dma((2, 2, NR)), dma((2, 2, NR)), dma((2, 2, NR)), dma((2, 2, NR)),
            dma((2, 8)), dma((N,)), dma((N,)), dma((N,)), dma((N,)),
        ],
        compiler_params=pltpu.CompilerParams(collective_id=2, has_side_effects=True, vmem_limit_bytes=60 * 2**20),
        name='mlp',
    )(o, hidden, gain, wo, wg, wu, wd)


def solution(mesh):
    width_shards = mesh.shape['dm']
    row_spec = P('dp', 'dm')
    cache_spec = P(('dp', 'dm'), None, 'tp', None)
    batch_spec = P(('dp', 'dm'))
    rope_spec = P(('dp', 'dm'), None)
    in_specs = (row_spec, P('dm', 'tp', None), P('dm', 'tp', None), P('dm', 'tp', None), P('tp', None, 'dm'), P('dm', 'tp'), P('dm', 'tp'), P('tp', 'dm'), P('dm'), P('dm'), cache_spec, cache_spec, batch_spec, rope_spec, rope_spec)
    out_specs = (row_spec, cache_spec, cache_spec)

    def local_layer(hidden, w_q, w_k, w_v, w_o, w_gate, w_up, w_down, norm_attn, norm_mlp, k_cache, v_cache, seq_lens, rope_cos, rope_sin):
        width_full = hidden.shape[1] * width_shards
        x_norm = norm_call(hidden, norm_attn.reshape(1, -1), width_full)
        q_part = jnp.einsum('bd,dhk->hbk', x_norm, w_q, preferred_element_type=F32)
        k_part = jnp.einsum('bd,dhk->hbk', x_norm, w_k, preferred_element_type=F32)
        v_part = jnp.einsum('bd,dhk->hbk', x_norm, w_v, preferred_element_type=F32)
        q_rot, kv_new = rope_call(q_part, jnp.concatenate([k_part, v_part], axis=0), rope_cos, rope_sin)
        k_out, v_out, o = attn_call(q_rot, kv_new, seq_lens, k_cache.reshape(64, 256, 128), v_cache.reshape(64, 256, 128))
        h_out = mlp_call(o, hidden, norm_mlp.reshape(1, -1), w_o.reshape(-1, w_o.shape[-1]), w_gate, w_up, w_down, width_full)
        return h_out, k_out.reshape(k_cache.shape), v_out.reshape(v_cache.shape)

    return jax.shard_map(local_layer, mesh=mesh, in_specs=in_specs, out_specs=out_specs, check_vma=False)
```

time: 375 us -> 199 us (0.53)
  Pallas kernels: 0 us -> 181 us
  waiting for transfers between devices: 145 us -> 0 us
  blocking collectives: 102 us -> 0 us
  matrix products: 88 us -> 10.3 us
  other arithmetic: 24.1 us -> 0.02 us
  between operations: 14 us -> 0.81 us
  local copies, waits for them, and re-layouts: 0.54 us -> 6.42 us
    pallas_call x0 -> x4, Pallas kernels: none -> 181 us  [the longest x1 136 us: mlp_call(): pl.pallas_call(functools.partial(mlp_kernel, width_full), out_shape=jax.S...]
    psum x1 -> x0, waiting for transfers between devices: 134 us -> none  [local_layer(): lax.psum(jnp.dot(x_mlp, w_up, preferred_element_type=jnp.float32), 'dm')]
    psum x4 -> x0, blocking collectives: 93.7 us -> none  [the longest x1 41.8 us: local_layer(): lax.psum(jnp.dot(gated_act, w_down, preferred_element_type=jnp.float32),...]
    dot_general x8 -> x3, matrix products: 83.2 us -> 10.3 us  [the longest x1 9.37 us: local_layer(): q_part = jnp.einsum('bd,dhk->hbk', x_norm, w_q, preferred_element_type=F32)]
    select_n x1 -> x0, other arithmetic: 13.8 us -> none  [attend(): k_out = jnp.where(write_mask, k_rot[:, None], k_cache)]
    reduce_scatter x3 -> x0, waiting for transfers between devices: 11.3 us -> none  [the longest x1 5.68 us: local_layer(): q_rows = lax.psum_scatter(q_part, 'dm', scatter_dimension=0, tiled=True)]
    all_gather x1 -> x0, blocking collectives: 8.46 us -> none  [local_layer(): heads_all = lax.all_gather(attn_heads, 'dm', axis=0, tiled=True)]
    sub x1 -> x0, matrix products: 4.7 us -> none  [attend(): attn_probs = jax.nn.softmax(scores, axis=-1).astype(jnp.bfloat16)]
  transfers between devices with their start and end apart: 4 -> 0, of which waited for: 3 -> 0; matrix products, arithmetic and copies ran while one was open for 8% -> 0% of each run, Pallas kernels for 0% -> 0%
where the time goes in v1:
time: 199 us
  Pallas kernels  181 us (91%)
  matrix products  10.3 us (5%)
  local copies, waits for them, and re-layouts  6.42 us (3%)
    pallas_call x1, Pallas kernels, mlp_call(): pl.pallas_call(functools.partial(mlp_kernel, width_full), out_shape=jax.S...  136 us
    pallas_call x1, Pallas kernels, attn_call(): pl.pallas_call(attn_kernel, out_shape=(cache, cache, jax.ShapeDtypeStruct...  23.5 us
    pallas_call x1, Pallas kernels, rope_call(): pl.pallas_call(rope_kernel, out_shape=(jax.ShapeDtypeStruct((16, 64, 128)...  15.9 us
    dot_general x1, matrix products, local_layer(): q_part = jnp.einsum('bd,dhk->hbk', x_norm, w_q, preferred_element_type=F32)  9.37 us
    pallas_call x1, Pallas kernels, norm_call(): pl.pallas_call(functools.partial(norm_kernel, width_full), out_shape=jax....  5.72 us
    unnamed x21, local copies, waits for them, and re-layouts  4.26 us

profile of v1, /device:TPU:0, one launch (start us, length us, event | category | flops | bytes accessed | tf_op | source)
XLA Modules:
  0.0 199.0 jit_solution(1714242196768013462)
XLA Ops:
  0.6 0.0 copy-start
  0.6 0.9 reshape.27.g_ref
  1.5 1.3 reshape.30.gain
  2.8 0.0 copy-start.2
  2.8 1.2 copy-done.2
  4.0 0.0 copy-start.9
  4.0 5.7 %norm_x.1 = bf16[128,4096]{1,0:T(8,128)(2,1)S(1)} custom-call(bf16[128,4096]{1,0:T(8,128)(2,1)S(1)} %copy-done.2, bf16[1,4096]{1,0:T(2,128)(2,1)S(1)} %reshape.27.g_ref), custom_call_target="tpu_custom_call" | custom-call | tf_op jit(solution)/shard_map/norm_x/pallas_call | solution.py:50
  9.8 0.0 copy-done
  9.8 0.5 fusion.9
  10.3 0.0 copy-done.9
  10.3 0.5 fusion.12
  10.7 0.0 copy-start.6
  10.8 0.0 copy-start.7
  10.8 0.0 copy-start.3
  10.8 0.0 copy-start.4
  10.8 0.0 copy-start.8
  10.8 9.4 %fusion.6.q_ref = f32[16,128,128]{2,1,0:T(8,128)S(1)} fusion(bf16[4096,16,128]{2,1,0:T(8,128)(2,1)} %param.16, bf16[128,4096]{1,0:T(8,128)(2,1)S(1)} %norm_x.1), kind=kOutput, calls=%fused_computation.6 | convolution fusion | flops 2147483648 | bytes 18874368 | tf_op jit(solution)/shard_map/bd,dhk->hbk/dot_general | solution.py:515
  20.2 0.0 copy-done.6
  20.2 0.0 copy-done.7
  20.2 15.9 %rs_rope.1 = (bf16[16,64,128]{2,1,0:T(8,128)(2,1)S(1)}, bf16[4,64,128]{2,1,0:T(8,128)(2,1)S(1)}) custom-call(f32[16,128,128]{2,1,0:T(8,128)S(1)} %fusion.6.q_ref, f32[4,128,128]{2,1,0:T(8,128)S(1)} %pad_maximum_fusion.kv_ref, f32[64,64]{1,0:T(8,128)S(1)} %copy-done.6, f32[64,64]{1,0:T(8,128)S(1)} %copy-done.7), custom_call_target="tpu_custom_call" | custom-call | tf_op jit(solution)/shard_map/rs_rope/pallas_call | solution.py:100
  36.1 0.0 copy-done.3
  36.1 0.0 copy-done.4
  36.2 0.0 copy-done.8
  36.2 23.5 %attend.1 = (bf16[64,256,128]{2,1,0:T(8,128)(2,1)}, bf16[64,256,128]{2,1,0:T(8,128)(2,1)}, bf16[64,2048]{1,0:T(8,128)(2,1)S(1)}) custom-call(bf16[16,64,128]{2,1,0:T(8,128)(2,1)S(1)} %get-tuple-element.8.q_ref, bf16[4,64,128]{2,1,0:T(8,128)(2,1)S(1)} %get-tuple-element.9.kv_ref, s32[64]{0:T(128)S(1)} %copy-done.8, bf16[64,256,128]{2,1,0:T(8,128)(2,1)S(1)} %bitcast.18, ...), custom_call_target="tpu_custom_call" | custom-call | tf_op jit(solution)/shard_map/attend/pallas_call | solution.py:171
  59.7 0.0 copy-start.5
  59.7 0.7 copy-done.5
  60.4 0.0 copy-start.1
  60.4 136.3 %mlp.1 = bf16[128,4096]{1,0:T(8,128)(2,1)} custom-call(bf16[64,2048]{1,0:T(8,128)(2,1)} %copy-done.5, bf16[128,4096]{1,0:T(8,128)(2,1)} %hid.1, bf16[1,4096]{1,0:T(2,128)(2,1)} %reshape.30.gain, bf16[2048,4096]{1,0:T(8,128)(2,1)} %bitcast.20, bf16[4096,5504]{1,0:T(8,128)(2,1)} %wg.1, bf16[4096,5504]{1,0:T(8,128)(2,1)} %wu.1, bf16[5504,4096]{1,0:T(8,128)(2,1)} %wd.1), custom_call_target="tpu_custom_call" | custom-call | tf_op jit(solution)/shard_map/mlp/pallas_call | solution.py:474
  196.8 2.3 %copy.34 = bf16[128,4096]{1,0:T(8,128)(2,1)} copy(bf16[128,4096]{1,0:T(8,128)(2,1)} %mlp.1) | data formatting | bytes 2097152
  199.0 0.0 copy-done.1
  (1 shorter events, 0.0 us)
Async XLA Ops:
  0.6 9.1 %copy-start = (bf16[4096,2,128]{2,1,0:T(2,128)(2,1)S(1)}, bf16[4096,2,128]{2,1,0:T(2,128)(2,1)}, u32[]{:S(2)}) copy-start(bf16[4096,2,128]{2,1,0:T(2,128)(2,1)} %param.17) | copy-start | bytes 6291460
  2.8 1.2 copy-start.2
  4.0 6.2 %copy-start.9 = (bf16[4096,2,128]{2,1,0:T(2,128)(2,1)S(1)}, bf16[4096,2,128]{2,1,0:T(2,128)(2,1)}, u32[]{:S(2)}) copy-start(bf16[4096,2,128]{2,1,0:T(2,128)(2,1)} %param.18) | copy-start | bytes 6291460
  10.7 9.5 %copy-start.6 = (f32[64,64]{1,0:T(8,128)S(1)}, f32[64,64]{1,0:T(8,128)}, u32[]{:S(2)}) copy-start(f32[64,64]{1,0:T(8,128)} %cos_ref.1) | copy-start | bytes 49156
  10.8 9.5 %copy-start.7 = (f32[64,64]{1,0:T(8,128)S(1)}, f32[64,64]{1,0:T(8,128)}, u32[]{:S(2)}) copy-start(f32[64,64]{1,0:T(8,128)} %sin_ref.1) | copy-start | bytes 49156
  10.8 25.4 %copy-start.3 = (bf16[64,128,2,128]{3,2,1,0:T(2,128)(2,1)S(1)}, bf16[64,128,2,128]{3,2,1,0:T(2,128)(2,1)}, u32[]{:S(2)}) copy-start(bf16[64,128,2,128]{3,2,1,0:T(2,128)(2,1)} %param.25) | copy-start | bytes 12582916
  10.8 25.4 %copy-start.4 = (bf16[64,128,2,128]{3,2,1,0:T(2,128)(2,1)S(1)}, bf16[64,128,2,128]{3,2,1,0:T(2,128)(2,1)}, u32[]{:S(2)}) copy-start(bf16[64,128,2,128]{3,2,1,0:T(2,128)(2,1)} %param.26) | copy-start | bytes 12582916
  10.8 25.4 %copy-start.8 = (s32[64]{0:T(128)S(1)}, s32[64]{0:T(128)}, u32[]{:S(2)}) copy-start(s32[64]{0:T(128)} %len_ref.1) | copy-start | bytes 772
  59.7 0.7 copy-start.5
  60.4 138.6 %copy-start.1 = (bf16[4096,2,128]{2,1,0:T(2,128)(2,1)S(1)}, bf16[4096,2,128]{2,1,0:T(2,128)(2,1)}, u32[]{:S(2)}) copy-start(bf16[4096,2,128]{2,1,0:T(2,128)(2,1)} %param.17) | copy-start | bytes 6291460

commit v2 on v0

v2 whole, which is shorter than its diff:
```python
import functools

import jax
import jax.numpy as jnp
from jax import lax
from jax.experimental import pallas as pl
from jax.experimental.pallas import tpu as pltpu
from jax.sharding import PartitionSpec as P

EPS = 1e-6
MESH = pl.DeviceIdType.MESH
F32 = jnp.float32
BF16 = jnp.bfloat16
ANY = pl.BlockSpec(memory_space=pl.ANY)
VM = pl.BlockSpec(memory_space=pltpu.VMEM)
HB = pl.BlockSpec(memory_space=pltpu.HBM)
SM = pl.BlockSpec(memory_space=pltpu.SMEM)


def me():
    return lax.axis_index('dp'), lax.axis_index('dm'), lax.axis_index('tp')


def row_to_lanes(col):
    return jnp.broadcast_to(col, (128, 128)).T[0:8, :]


def lanes_to_row(vec):
    return jnp.broadcast_to(vec, (128, 128)).T[:, 0:1]


KC = 8
VLIM = 55
PAIRS = 10


def qkv_kernel(width_full, h_hbm, g_hbm, cos_hbm, sin_hbm, wq, wk, wv, qo_ref, kvo_ref,
               h_ref, g_ref, cos_ref, sin_ref, insem, rawq, rawkv, wall, x_s, part, rbuf, mine_st, their_st, qsem, kvsem, ss, rs, stsem):
    dp, dm, tp = me()
    peer = (dp, 1 - dm, tp)
    mine = pl.ds(pl.multiple_of(dm * 64, 64), 64)
    other = pl.ds(pl.multiple_of((1 - dm) * 64, 64), 64)
    qrows = 65536 // KC

    def kvcopy(t):
        return pltpu.make_async_copy((wk, wv)[t], rawkv.at[t], kvsem.at[t])

    def qcopy(j):
        rows = pl.ds(pl.multiple_of(j * qrows, qrows), qrows)
        return pltpu.make_async_copy(wq.at[rows], rawq.at[rows], qsem.at[j])

    ins = [pltpu.make_async_copy(a, b, insem.at[i]) for i, (a, b) in enumerate(((h_hbm, h_ref), (g_hbm, g_ref), (cos_hbm, cos_ref), (sin_hbm, sin_ref)))]
    for cp in ins:
        cp.start()
    for t in range(2):
        kvcopy(t).start()
    for j in range(KC):
        qcopy(j).start()
    bar = pltpu.get_barrier_semaphore()
    pl.semaphore_signal(bar, inc=1, device_id=peer, device_id_type=MESH)
    ins[0].wait()
    sq = jnp.zeros((128, 128), F32)
    for j in range(32):
        h = h_ref[:, 128 * j:128 * j + 128].astype(F32)
        sq += h * h
    mine_st[...] = row_to_lanes(jnp.sum(sq, axis=-1, keepdims=True))
    pl.semaphore_wait(bar, 1)
    stat = pltpu.make_async_remote_copy(mine_st, their_st, stsem.at[0], stsem.at[1], device_id=peer, device_id_type=MESH)
    stat.start()

    r_i = lax.broadcasted_iota(jnp.int32, (256, 256), 0)
    c_i = lax.broadcasted_iota(jnp.int32, (256, 256), 1)
    perm_kv = jnp.where(c_i == 2 * lax.rem(r_i, 128) + r_i // 128, 1.0, 0.0).astype(BF16)
    for t in range(2):
        kvcopy(t).wait()

    @pl.loop(0, 8)
    def _(j):
        for i in range(4):
            at = pl.ds(pl.multiple_of(j * 1024 + i * 256, 256), 256)
            to = pl.ds(pl.multiple_of(j * 512 + i * 128, 128), 128)
            d = jnp.dot(perm_kv, jnp.concatenate([rawkv[0, at, :], rawkv[1, at, :]], axis=1), preferred_element_type=F32).astype(BF16)
            wall[0, to, :] = d[0:128]
            wall[1, to, :] = d[128:256]

    stat.wait()
    ins[1].wait()
    scale = lax.rsqrt(lanes_to_row(mine_st[0:1, :] + their_st[0:1, :]) / width_full + EPS)
    for j in range(32):
        cols = slice(128 * j, 128 * j + 128)
        x_s[:, cols] = (h_ref[:, cols].astype(F32) * scale * g_ref[j:j + 1, :].astype(F32)).astype(BF16)

    def send(i):
        return pltpu.make_async_remote_copy(part.at[i, other, :], rbuf.at[i], ss.at[i], rs.at[i], device_id=peer, device_id_type=MESH)

    def product(i):
        part[i] = jnp.dot(x_s[...], wall[i], preferred_element_type=F32)
        send(i).start()

    @pl.loop(0, 2)
    def _(i):
        product(i)

    r_h = lax.broadcasted_iota(jnp.int32, (128, 256), 0)
    c_h = lax.broadcasted_iota(jnp.int32, (128, 256), 1)
    for half in range(2):
        perm_q = jnp.where(c_h == 16 * lax.rem(r_h, 16) + r_h // 16 + 8 * half, 1.0, 0.0).astype(BF16)

        @pl.loop(0, KC)
        def _(j):
            if half == 0:
                qcopy(j).wait()
            n = qrows // 512
            for i in range(n):
                a0 = pl.ds(pl.multiple_of(j * qrows + i * 512, 256), 256)
                a1 = pl.ds(pl.multiple_of(j * qrows + i * 512 + 256, 256), 256)
                to = pl.ds(pl.multiple_of((j * n + i) * 32, 32), 32)
                d = jnp.dot(perm_q, jnp.concatenate([rawq[a0, :], rawq[a1, :]], axis=1), preferred_element_type=F32).astype(BF16)
                for h in range(8):
                    rows = slice(16 * h, 16 * h + 16)
                    wall[2 + 4 * half + h // 2, to, (h % 2) * 128:(h % 2) * 128 + 128] = jnp.concatenate([d[rows, 0:128], d[rows, 128:256]], axis=0)

        @pl.loop(2 + 4 * half, 6 + 4 * half)
        def _(i):
            product(i)

    ins[2].wait()
    ins[3].wait()
    c = cos_ref[...]
    s = sin_ref[...]
    cos2 = jnp.concatenate([c, c], axis=-1)
    sin2 = jnp.concatenate([-s, s], axis=-1)

    def rope(a):
        return (a * cos2 + pltpu.roll(a, 64, 1) * sin2).astype(BF16)

    for i in range(PAIRS):
        send(i).wait_recv()
        lo = part[i, mine, 0:128] + rbuf[i, :, 0:128]
        hi = part[i, mine, 128:256] + rbuf[i, :, 128:256]
        if i < 2:
            kvo_ref[i] = rope(lo)
            kvo_ref[2 + i] = hi.astype(BF16)
        else:
            qo_ref[2 * i - 4] = rope(lo)
            qo_ref[2 * i - 3] = rope(hi)
    for i in range(PAIRS):
        send(i).wait_send()


def qkv_call(hidden, gain, cos, sin, wq, wk, wv, width_full):
    dma = pltpu.SemaphoreType.DMA
    return pl.pallas_call(
        functools.partial(qkv_kernel, width_full),
        out_shape=(jax.ShapeDtypeStruct((16, 64, 128), BF16), jax.ShapeDtypeStruct((4, 64, 128), BF16)),
        in_specs=[HB] * 7, out_specs=(VM, VM),
        scratch_shapes=[
            pltpu.VMEM((128, 4096), BF16), pltpu.VMEM((32, 128), BF16), pltpu.VMEM((64, 64), F32), pltpu.VMEM((64, 64), F32), dma((4,)),
            pltpu.VMEM((65536, 128), BF16),
            pltpu.VMEM((2, 8192, 128), BF16),
            pltpu.VMEM((PAIRS, 4096, 256), BF16),
            pltpu.VMEM((128, 4096), BF16),
            pltpu.VMEM((PAIRS, 128, 256), F32),
            pltpu.VMEM((PAIRS, 64, 256), F32),
            pltpu.VMEM((8, 128), F32), pltpu.VMEM((8, 128), F32),
            dma((KC,)), dma((2,)), dma((PAIRS,)), dma((PAIRS,)), dma((2,)),
        ],
        compiler_params=pltpu.CompilerParams(collective_id=0, has_side_effects=True, vmem_limit_bytes=VLIM * 2**20),
        name='qkv',
    )(hidden, gain, cos, sin, wq, wk, wv)


ACH = 4
AROWS = 64 // ACH


def attn_kernel(q_ref, kv_ref, len_ref, kc, vc, ko, vo, o_hbm, kb, vb, qs, os, o_ref, isem, osem, obsem):
    def cin(ch, t):
        rows = pl.ds(ch * AROWS, AROWS)
        return pltpu.make_async_copy((kc, vc)[t].at[rows], (kb, vb)[t].at[rows], isem.at[t, ch])

    def cout(ch, t):
        rows = pl.ds(ch * AROWS, AROWS)
        return pltpu.make_async_copy((kb, vb)[t].at[rows], (ko, vo)[t].at[rows], osem.at[t, ch])

    for ch in range(ACH):
        for t in range(2):
            cin(ch, t).start()
    for h in range(16):
        qs[pl.ds(h, 64, stride=16), :] = q_ref[h].astype(F32)
    row16 = lax.broadcasted_iota(jnp.int32, (16, 128), 0)
    col = lax.broadcasted_iota(jnp.int32, (16, 256), 1)
    head = lax.broadcasted_iota(jnp.int32, (16, 256), 0)
    own = lax.rem(col, 2) == head // 8

    @pl.loop(0, ACH)
    def _(ch):
        cin(ch, 0).wait()
        cin(ch, 1).wait()
        kv32 = [kv_ref[j, pl.ds(pl.multiple_of(ch * AROWS, AROWS), AROWS), :].astype(F32) for j in range(4)]
        for i in range(AROWS):
            b = ch * AROWS + i
            ln = len_ref[b]
            t8 = ln // 8
            at = pl.ds(pl.multiple_of(t8 * 16, 16), 16)
            r0 = 2 * (ln - 8 * t8)
            for t, buf in enumerate((kb, vb)):
                old = buf[b, at, :].astype(F32)
                n0 = jnp.broadcast_to(kv32[2 * t][i:i + 1, :], (16, 128))
                n1 = jnp.broadcast_to(kv32[2 * t + 1][i:i + 1, :], (16, 128))
                new = jnp.where(row16 == r0, n0, jnp.where(row16 == r0 + 1, n1, old))
                buf[b, at, :] = new.astype(BF16)
        cout(ch, 0).start()
        cout(ch, 1).start()
        sc = []
        for i in range(AROWS):
            b = ch * AROWS + i
            q = qs[pl.ds(pl.multiple_of(b * 16, 16), 16), :].astype(BF16)
            sc.append(lax.dot_general(q, kb[b], (((1,), (1,)), ((), ())), preferred_element_type=F32))
        pr = []
        for i in range(AROWS):
            ln = len_ref[ch * AROWS + i]
            s = jnp.where(own & (col <= 2 * ln + 1), sc[i] * (128.0 ** -0.5), -1e30)
            p = jnp.exp(s - jnp.max(s, axis=-1, keepdims=True))
            pr.append((p / jnp.sum(p, axis=-1, keepdims=True)).astype(BF16))
        for i in range(AROWS):
            b = ch * AROWS + i
            os[pl.ds(pl.multiple_of(b * 16, 16), 16), :] = jnp.dot(pr[i], vb[b], preferred_element_type=F32)

    for h in range(16):
        o_ref[:, h * 128:(h + 1) * 128] = os[pl.ds(h, 64, stride=16), :].astype(BF16)
    ocp = pltpu.make_async_copy(o_ref, o_hbm, obsem)
    ocp.start()
    for ch in range(ACH):
        cout(ch, 0).wait()
        cout(ch, 1).wait()
    ocp.wait()


def attn_call(q_rot, kv_new, seq_lens, k_cache, v_cache):
    cache = jax.ShapeDtypeStruct((64, 256, 128), BF16)
    return pl.pallas_call(
        attn_kernel,
        out_shape=(cache, cache, jax.ShapeDtypeStruct((64, 2048), BF16)),
        in_specs=[VM, VM, SM, ANY, ANY], out_specs=(ANY, ANY, HB),
        scratch_shapes=[pltpu.VMEM((64, 256, 128), BF16), pltpu.VMEM((64, 256, 128), BF16), pltpu.VMEM((1024, 128), F32), pltpu.VMEM((1024, 128), F32), pltpu.VMEM((64, 2048), BF16),
                        pltpu.SemaphoreType.DMA((2, ACH)), pltpu.SemaphoreType.DMA((2, ACH)), pltpu.SemaphoreType.DMA],
        compiler_params=pltpu.CompilerParams(vmem_limit_bytes=32 * 2**20),
        name='attend',
    )(q_rot, kv_new, seq_lens, k_cache, v_cache)


C = 256
N = 22
NB = 4
ND = 8
NR = 4
RB = 128 // NR
LEAD = 5
LAG = 2
DLAG = 5


def mlp_kernel(width_full, o_hbm, hid_hbm, gain_hbm, wo, wg, wu, wd, out,
               o_ref, hid, gain, insem, wbuf, dbuf, oall, acc, dd, xs, xr, hq, oq, x2, gown, gsnd, grcv, mall, st,
               wsem, dsem, osem, d2d, xx, agc, agx, fwd, stsem, gs, gr, ms, mr):
    dp, dm, tp = me()
    x = tp // 2
    c = lax.rem(tp, 2)
    ypeer = (dp, 1 - dm, tp)
    cpeer = (dp, dm, x * 2 + 1 - c)
    xpeer = (dp, dm, (1 - x) * 2 + c)
    flat = dm * 4 + tp

    def at_flat(k):
        f = lax.rem(flat + k, 8)
        return f, (dp, f // 4, lax.rem(f, 4))

    def rdma(src, dst, s, r, dev):
        return pltpu.make_async_remote_copy(src, dst, s, r, device_id=dev, device_id_type=MESH)

    def blk(r):
        return slice(r * RB, (r + 1) * RB)

    def rows_of(r):
        return pl.ds(pl.multiple_of((dm if r % 2 == 0 else 1 - dm) * 64 + (r // 2) * RB, RB), RB)

    def bchunk(t):
        return jnp.where(t < N - LEAD, t + LEAD, t - (N - LEAD))

    BODD = 2 * N - LEAD

    def col(ch):
        return pl.multiple_of(ch * C - 128, 128)

    def wcopy(s, ch, t):
        slot = lax.rem(s, NB)
        return pltpu.make_async_copy((wg, wu)[t].at[:, pl.ds(col(ch), C)], wbuf.at[slot, t], wsem.at[slot, t])

    def wcopy0(s, t):
        slot = s % NB
        return pltpu.make_async_copy((wg, wu)[t].at[:, 0:128], wbuf.at[slot, t, :, 0:128], wsem.at[slot, t])

    def opiece(n):
        return (1 - x) * 4 + n if n < 4 else x * 4 + n - 4

    def ocopy(n):
        cols = pl.ds(pl.multiple_of(opiece(n) * 512, 512), 512)
        return pltpu.make_async_copy(wo.at[:, :, cols], dbuf.at[:, :, cols], dsem.at[n])

    def dcopy(d, ch):
        slot = lax.rem(d, ND)
        return pltpu.make_async_copy(wd.at[pl.ds(col(ch), C)], dbuf.at[slot], dsem.at[slot])

    def dcopy0(d):
        slot = d % ND
        return pltpu.make_async_copy(wd.at[0:128], dbuf.at[slot, 0:128], dsem.at[slot])

    ins = [pltpu.make_async_copy(a, b, insem.at[i]) for i, (a, b) in enumerate(((o_hbm, o_ref), (hid_hbm, hid), (gain_hbm, gain)))]
    ins[0].start()
    for j in range(8):
        ocopy(j).start()
    ins[1].start()
    ins[2].start()

    bar = pltpu.get_barrier_semaphore()
    for k in range(1, 8):
        pl.semaphore_signal(bar, inc=1, device_id=at_flat(k)[1], device_id_type=MESH)
    pl.semaphore_wait(bar, 7)

    def ocp(b):
        return rdma(o_ref.at[blk(b)], oall.at[blk(b)], osem.at[0, b], osem.at[1, b], ypeer)

    ins[0].wait()
    ocp(0).start()
    ocp(1).start()

    def d2d_cp(u, p, r):
        xq = 1 - x if p == 0 else x
        return rdma(acc.at[1 - c, xq, blk(r), :], dd.at[xq, blk(r), :], d2d.at[u, p, 0, r], d2d.at[u, p, 1, r], cpeer)

    def x_cp(u, r):
        return rdma(xs.at[blk(r)], xr.at[blk(r)], xx.at[u, 0, r], xx.at[u, 1, r], xpeer)

    def agc_cp(u, r, buf):
        return rdma(buf.at[tp, blk(r)], buf.at[tp, blk(r)], agc.at[u, 0, r], agc.at[u, 1, r], cpeer)

    def agx_cp(u, r, buf):
        return rdma(buf.at[tp, blk(r)], buf.at[tp, blk(r)], agx.at[u, 0, r], agx.at[u, 1, r], xpeer)

    def fwd_cp(u, r, buf):
        q = lax.rem(tp + 2, 4)
        return rdma(buf.at[q, blk(r)], buf.at[q, blk(r)], fwd.at[u, 0, r], fwd.at[u, 1, r], cpeer)

    def chip_sum(u, r):
        d2d_cp(u, 0, r).wait_recv()
        xs[blk(r), :] = acc[c, 1 - x, blk(r), :] + dd[1 - x, blk(r), :]
        x_cp(u, r).start()

    def total(u, r):
        d2d_cp(u, 1, r).wait_recv()
        x_cp(u, r).wait_recv()
        return (acc[c, x, blk(r), :] + dd[x, blk(r), :] + xr[blk(r), :]).astype(BF16)

    def gather(u, r, buf):
        agx_cp(u, r, buf).start()
        agc_cp(u, r, buf).start()

    def relay(u, r, buf):
        agx_cp(u, r, buf).wait_recv()
        fwd_cp(u, r, buf).start()

    def arrived(u, r, buf):
        agc_cp(u, r, buf).wait_recv()
        fwd_cp(u, r, buf).wait_recv()

    def drained(u, r, buf):
        d2d_cp(u, 0, r).wait_send()
        d2d_cp(u, 1, r).wait_send()
        x_cp(u, r).wait_send()
        agc_cp(u, r, buf).wait_send()
        agx_cp(u, r, buf).wait_send()
        fwd_cp(u, r, buf).wait_send()

    def zero_acc():
        for a in range(2):
            for b in range(2):
                acc[a, b] = jnp.zeros((128, 1024), F32)

    def acc_cols(n):
        q = n // 2
        return q % 2, q // 2, slice((n % 2) * 512, (n % 2) * 512 + 512)

    def wo_piece(src, n, rs):
        at = opiece(n)
        cols = pl.ds(pl.multiple_of(at * 512, 512), 512)
        v = jnp.dot(src[:, 0:C], dbuf[0, :, cols], preferred_element_type=F32)
        for j in range(1, 8):
            v += jnp.dot(src[:, j * C:(j + 1) * C], dbuf[j, :, cols], preferred_element_type=F32)
        q = at // 2
        for i, r in enumerate(rs):
            acc[lax.rem(q, 2), q // 2, blk(r), (n % 2) * 512:(n % 2) * 512 + 512] = v[i * RB:i * RB + RB]

    def own(ns):
        for n in ns:
            ocopy(n).wait()
            wo_piece(o_ref, n, (0, 2))

    def peers(r, ns):
        for n in ns:
            wo_piece(oall.at[blk(r // 2)], n, (r,))

    own(range(4))
    d2d_cp(0, 0, 0).start()
    d2d_cp(0, 0, 2).start()
    own((4, 5))
    chip_sum(0, 0)
    own((6, 7))
    d2d_cp(0, 1, 0).start()
    d2d_cp(0, 1, 2).start()
    for t in range(2):
        wcopy0(0, t).start()
    for s in range(1, NB):
        for t in range(2):
            wcopy(s, s, t).start()
    ocp(0).wait_recv()
    peers(1, range(4))
    d2d_cp(0, 0, 1).start()
    peers(1, (4, 5))
    chip_sum(0, 1)
    peers(1, (6, 7))
    d2d_cp(0, 1, 1).start()
    ins[1].wait()
    ins[2].wait()
    qcols = pl.ds(pl.multiple_of(tp * 1024, 1024), 1024)

    def h_mid(r):
        att = total(0, r)
        h1 = (hid[rows_of(r), qcols].astype(F32) + att.astype(F32)).astype(BF16)
        hq[tp, blk(r)] = h1
        gather(0, r, hq)
        h32 = h1.astype(F32)
        return jnp.sum(h32 * h32, axis=-1, keepdims=True)

    def st_cp(b, k, own):
        f, dev = at_flat(k)
        if own:
            return rdma(st.at[b, flat], st.at[b, flat], stsem.at[b, 0, f], stsem.at[b, 1, flat], dev)
        return rdma(st.at[b, f], st.at[b, f], stsem.at[b, 0, f], stsem.at[b, 1, f], dev)

    def stats(b, sq):
        st[b, flat] = row_to_lanes(jnp.concatenate(sq + [jnp.zeros((64, 1), F32)], axis=0))
        for k in range(1, 8):
            st_cp(b, k, True).start()

    lane = lax.broadcasted_iota(jnp.int32, (8, 128), 1)

    def x2_rows(b):
        for k in range(1, 8):
            st_cp(b, k, False).wait_recv()
        tot = jnp.zeros((8, 128), F32)
        for f in range(8):
            v = st[b, f]
            swapped = jnp.where(lane < RB, pltpu.roll(v, 128 - RB, 1), pltpu.roll(v, RB, 1))
            tot += jnp.where(dm == f // 4, v, swapped)
        scale = lax.rsqrt(lanes_to_row(tot[0:1, :]) / width_full + EPS)[0:64]
        rows = slice(64 * b, 64 * b + 64)
        arrived(0, 2 * b, hq)
        arrived(0, 2 * b + 1, hq)
        for j in range(32):
            x2[rows, 128 * j:128 * j + 128] = (hq[j // 8, rows, 128 * (j % 8):128 * (j % 8) + 128].astype(F32) * scale * gain[j:j + 1, :].astype(F32)).astype(BF16)

    sq0 = h_mid(0)
    ocp(1).wait_recv()
    peers(3, range(4))
    d2d_cp(0, 0, 3).start()
    peers(3, (4, 5))
    stats(0, [sq0, h_mid(1)])
    chip_sum(0, 2)
    peers(3, (6, 7))
    d2d_cp(0, 1, 3).start()
    dcopy0(0).start()
    for d in range(1, ND):
        dcopy(d, d).start()
    relay(0, 0, hq)
    chip_sum(0, 3)
    relay(0, 1, hq)
    x2_rows(0)

    def g_cp(b, ch, w=C):
        return rdma(gsnd.at[b, ch, :, :, 0:w], grcv.at[b, ch, :, :, 0:w], gs.at[b, ch], gr.at[b, ch], ypeer)

    def m_cp(b, ch, w=C):
        return rdma(mall.at[b, ch, 0:RB, 0:w], mall.at[b, ch, RB:2 * RB, 0:w], ms.at[b, ch], mr.at[b, ch], ypeer)

    def up_gate(ch, slot, blocks, w=C):
        lo, hi = blocks[0] * 64, blocks[-1] * 64 + 64
        for t in range(2):
            v = jnp.dot(x2[lo:hi, :], wbuf[slot, t, :, 0:w], preferred_element_type=F32)
            for i, b in enumerate(blocks):
                gown[b, ch, t, :, 0:w] = v[64 * i:64 * i + RB]
                gsnd[b, ch, t, :, 0:w] = v[64 * i + RB:64 * i + 64]

    def act(b, ch, w=C):
        g_cp(b, ch, w).wait_recv()
        g = gown[b, ch, 0, :, 0:w] + grcv[b, ch, 0, :, 0:w]
        u = gown[b, ch, 1, :, 0:w] + grcv[b, ch, 1, :, 0:w]
        mall[b, ch, 0:RB, 0:w] = (g * jax.nn.sigmoid(g) * u).astype(BF16)
        m_cp(b, ch, w).start()

    def down(b, ch, slot, w=C):
        m_cp(b, ch, w).wait_recv()
        m = mall[b, ch, :, 0:w]
        rows = pl.ds(pl.multiple_of(b * 64, 64), 64)

        for n in range(8):
            a, bb, cols = acc_cols(n)
            acc[a, bb, rows, cols] += jnp.dot(m, dbuf[slot, 0:w, n * 512:n * 512 + 512], preferred_element_type=F32)

    sqb = []

    def second_half(step):
        if step == 0:
            sqb.append(h_mid(2))
        elif step == 2:
            sqb.append(h_mid(3))
            stats(1, sqb)
        elif step == 3:
            relay(0, 2, hq)
            relay(0, 3, hq)
        elif step == LEAD - 1:
            x2_rows(1)
            for r in range(NR):
                drained(0, r, hq)
            zero_acc()

    for e in range(LEAD):
        for t in range(2):
            (wcopy0(0, t) if e == 0 else wcopy(e, e, t)).wait()
        up_gate(e, e % NB, [0], 128 if e == 0 else C)
        g_cp(0, e, 128 if e == 0 else C).start()
        for t in range(2):
            wcopy(e + NB, e + NB, t).start()
        if e >= LAG:
            act(0, e - LAG, 128 if e == LAG else C)
        second_half(e)

    def split(e):
        b = e // N
        return b, jnp.where(b == 0, e, bchunk(e - N))

    @pl.loop(LEAD, 2 * N + DLAG)
    def _(e):
        @pl.when(e < N)
        def _():
            for t in range(2):
                wcopy(e, e, t).wait()
            up_gate(e, lax.rem(e, NB), [0, 1])

        @pl.when(e == N)
        def _():
            for t in range(2):
                wcopy0(N, t).wait()
            up_gate(0, N % NB, [1], 128)

        @pl.when((e > N) & (e < N + LEAD))
        def _():
            for t in range(2):
                wcopy(e, e - N, t).wait()
            up_gate(e - N, lax.rem(e, NB), [1])

        @pl.when((e < 2 * N) & (e != BODD))
        def _():
            b, ch = split(e)
            g_cp(b, ch).start()

        @pl.when(e == BODD)
        def _():
            g_cp(1, 0, 128).start()

        s = e + NB

        @pl.when((s < N + LEAD) & (s != N))
        def _():
            for t in range(2):
                wcopy(s, jnp.where(s < N, s, s - N), t).start()

        @pl.when(s == N)
        def _():
            for t in range(2):
                wcopy0(N, t).start()

        i = e - LAG

        @pl.when((i < 2 * N) & (i != BODD))
        def _():
            b, ch = split(i)
            act(b, ch)

        @pl.when(i == BODD)
        def _():
            act(1, 0, 128)

        d = e - DLAG

        @pl.when(d == 0)
        def _():
            dcopy0(0).wait()
            down(0, 0, 0, 128)

        @pl.when(d == BODD)
        def _():
            dcopy0(BODD).wait()
            down(1, 0, BODD % ND, 128)

        @pl.when((d > 0) & (d != BODD))
        def _():
            b, ch = split(d)
            dcopy(d, ch).wait()
            down(b, ch, lax.rem(d, ND))

        f = d + ND

        @pl.when((f < 2 * N) & (f != BODD))
        def _():
            dcopy(f, split(f)[1]).start()

        @pl.when(f == BODD)
        def _():
            dcopy0(BODD).start()

        def res(r):
            mlp = total(1, r)
            oq[tp, blk(r)] = (hq[tp, blk(r)].astype(F32) + mlp.astype(F32)).astype(BF16)
            gather(1, r, oq)

        @pl.when(d == N)
        def _():
            for r in (0, 1):
                d2d_cp(1, 0, r).start()
                d2d_cp(1, 1, r).start()

        @pl.when(d == N + 1)
        def _():
            chip_sum(1, 0)
            chip_sum(1, 1)

        @pl.when(d == N + 5)
        def _():
            res(0)

        @pl.when(d == N + 7)
        def _():
            res(1)

        @pl.when(d == N + 10)
        def _():
            relay(1, 0, oq)
            relay(1, 1, oq)

    for r in (2, 3):
        d2d_cp(1, 0, r).start()
    for r in (2, 3):
        d2d_cp(1, 1, r).start()
    for r in (2, 3):
        chip_sum(1, r)
    for r in (2, 3):
        mlp = total(1, r)
        oq[tp, blk(r)] = (hq[tp, blk(r)].astype(F32) + mlp.astype(F32)).astype(BF16)
        gather(1, r, oq)
    for r in (2, 3):
        relay(1, r, oq)
    for b in range(2):
        for k in range(1, 8):
            st_cp(b, k, True).wait_send()
        ocp(b).wait_send()
        g_cp(b, 0, 128).wait_send()
        m_cp(b, 0, 128).wait_send()

    @pl.loop(1, N)
    def _(ch):
        for b in range(2):
            g_cp(b, ch).wait_send()
            m_cp(b, ch).wait_send()

    for r in range(NR):
        arrived(1, r, oq)
        for q in range(4):
            out[rows_of(r), 1024 * q:1024 * q + 1024] = oq[q, blk(r), :]
    for r in range(NR):
        drained(1, r, oq)


def mlp_call(o, hidden, gain, wo, wg, wu, wd, width_full):
    dma = pltpu.SemaphoreType.DMA
    return pl.pallas_call(
        functools.partial(mlp_kernel, width_full),
        out_shape=jax.ShapeDtypeStruct((128, 4096), BF16),
        in_specs=[HB] * 7, out_specs=VM,
        scratch_shapes=[
            pltpu.VMEM((64, 2048), BF16), pltpu.VMEM((128, 4096), BF16), pltpu.VMEM((32, 128), BF16), dma((3,)),
            pltpu.VMEM((NB, 2, 4096, C), BF16),
            pltpu.VMEM((ND, C, 4096), BF16),
            pltpu.VMEM((64, 2048), BF16),
            pltpu.VMEM((2, 2, 128, 1024), F32),
            pltpu.VMEM((2, 128, 1024), F32),
            pltpu.VMEM((128, 1024), F32),
            pltpu.VMEM((128, 1024), F32),
            pltpu.VMEM((4, 128, 1024), BF16),
            pltpu.VMEM((4, 128, 1024), BF16),
            pltpu.VMEM((128, 4096), BF16),
            pltpu.VMEM((2, N, 2, RB, C), F32),
            pltpu.VMEM((2, N, 2, RB, C), F32),
            pltpu.VMEM((2, N, 2, RB, C), F32),
            pltpu.VMEM((2, N, 2 * RB, C), BF16),
            pltpu.VMEM((2, 8, 8, 128), F32),
            dma((NB, 2)), dma((ND,)), dma((2, 2)),
            dma((2, 2, 2, NR)), dma((2, 2, NR)), dma((2, 2, NR)), dma((2, 2, NR)), dma((2, 2, NR)),
            dma((2, 2, 8)), dma((2, N)), dma((2, N)), dma((2, N)), dma((2, N)),
        ],
        compiler_params=pltpu.CompilerParams(collective_id=2, has_side_effects=True, vmem_limit_bytes=56 * 2**20),
        name='mlp',
    )(o, hidden, gain, wo, wg, wu, wd)


def solution(mesh):
    width_shards = mesh.shape['dm']
    row_spec = P('dp', 'dm')
    cache_spec = P(('dp', 'dm'), None, 'tp', None)
    batch_spec = P(('dp', 'dm'))
    rope_spec = P(('dp', 'dm'), None)
    in_specs = (row_spec, P('dm', 'tp', None), P('dm', 'tp', None), P('dm', 'tp', None), P('tp', None, 'dm'), P('dm', 'tp'), P('dm', 'tp'), P('tp', 'dm'), P('dm'), P('dm'), cache_spec, cache_spec, batch_spec, rope_spec, rope_spec)
    out_specs = (row_spec, cache_spec, cache_spec)

    def local_layer(hidden, w_q, w_k, w_v, w_o, w_gate, w_up, w_down, norm_attn, norm_mlp, k_cache, v_cache, seq_lens, rope_cos, rope_sin):
        width_full = hidden.shape[1] * width_shards
        q_rot, kv_new = qkv_call(hidden, norm_attn.reshape(-1, 128), rope_cos, rope_sin, w_q.reshape(-1, 128), w_k.reshape(-1, 128), w_v.reshape(-1, 128), width_full)
        k_out, v_out, o = attn_call(q_rot, kv_new, seq_lens, k_cache.reshape(64, 256, 128), v_cache.reshape(64, 256, 128))
        h_out = mlp_call(o, hidden, norm_mlp.reshape(-1, 128), w_o.reshape(8, 256, -1), w_gate, w_up, w_down, width_full)
        return h_out, k_out.reshape(k_cache.shape), v_out.reshape(v_cache.shape)

    return jax.shard_map(local_layer, mesh=mesh, in_specs=in_specs, out_specs=out_specs, check_vma=False)
```

time: 375 us -> 163 us (0.43)
  Pallas kernels: 0 us -> 157 us
  waiting for transfers between devices: 145 us -> 0 us
  blocking collectives: 102 us -> 0 us
  matrix products: 88 us -> 0 us
  other arithmetic: 24.1 us -> 0 us
  between operations: 14 us -> 0.72 us
  local copies, waits for them, and re-layouts: 0.54 us -> 4.78 us
    pallas_call x0 -> x3, Pallas kernels: none -> 157 us  [the longest x1 120 us: mlp_call(): pl.pallas_call(functools.partial(mlp_kernel, width_full), out_shape=jax.S...]
    psum x1 -> x0, waiting for transfers between devices: 134 us -> none  [local_layer(): lax.psum(jnp.dot(x_mlp, w_up, preferred_element_type=jnp.float32), 'dm')]
    psum x4 -> x0, blocking collectives: 93.7 us -> none  [the longest x1 41.8 us: local_layer(): lax.psum(jnp.dot(gated_act, w_down, preferred_element_type=jnp.float32),...]
    dot_general x8 -> x0, matrix products: 83.2 us -> none  [the longest x1 20.3 us: local_layer(): jnp.dot(gated_act, w_down, preferred_element_type=jnp.float32)]
    select_n x1 -> x0, other arithmetic: 13.8 us -> none  [attend(): k_out = jnp.where(write_mask, k_rot[:, None], k_cache)]
    reduce_scatter x3 -> x0, waiting for transfers between devices: 11.3 us -> none  [the longest x1 5.68 us: local_layer(): q_rows = lax.psum_scatter(q_part, 'dm', scatter_dimension=0, tiled=True)]
    all_gather x1 -> x0, blocking collectives: 8.46 us -> none  [local_layer(): heads_all = lax.all_gather(attn_heads, 'dm', axis=0, tiled=True)]
    unnamed x14 -> x13, local copies, waits for them, and re-layouts: 0.05 us -> 4.78 us
  transfers between devices with their start and end apart: 4 -> 0, of which waited for: 3 -> 0; matrix products, arithmetic and copies ran while one was open for 8% -> 0% of each run, Pallas kernels for 0% -> 0%
where the time goes in v2:
time: 163 us
  Pallas kernels  157 us (96%)
  local copies, waits for them, and re-layouts  4.78 us (3%)
    pallas_call x1, Pallas kernels, mlp_call(): pl.pallas_call(functools.partial(mlp_kernel, width_full), out_shape=jax.S...  120 us
    pallas_call x1, Pallas kernels, qkv_call(): pl.pallas_call(functools.partial(qkv_kernel, width_full), out_shape=(jax....  31.9 us
    pallas_call x1, Pallas kernels, attn_call(): pl.pallas_call(attn_kernel, out_shape=(cache, cache, jax.ShapeDtypeStruct...  5.64 us
    unnamed x13, local copies, waits for them, and re-layouts  4.78 us

profile of v2, /device:TPU:0, one launch (start us, length us, event | category | flops | bytes accessed | tf_op | source)
XLA Modules:
  0.0 162.6 jit_solution(10075148528170794124)
XLA Ops:
  0.6 0.0 copy-start
  0.6 0.0 copy-start.1
  0.7 0.0 copy-start.5
  0.7 31.9 %qkv.1 = (bf16[16,64,128]{2,1,0:T(8,128)(2,1)}, bf16[4,64,128]{2,1,0:T(8,128)(2,1)}) custom-call(bf16[128,4096]{1,0:T(8,128)(2,1)} %hid_hbm.1, bf16[32,128]{1,0:T(8,128)(2,1)} %bitcast.16, f32[64,64]{1,0:T(8,128)} %cos_hbm.1, f32[64,64]{1,0:T(8,128)} %sin_hbm.1, bf16[65536,128]{1,0:T(8,128)(2,1)} %bitcast.13, bf16[8192,128]{1,0:T(8,128)(2,1)} %bitcast.14, ...), custom_call_target="tpu_custom_call" | custom-call | tf_op jit(solution)/shard_map/qkv/pallas_call | solution.py:153
  32.5 0.0 copy-done
  32.5 0.0 copy-done.1
  32.5 0.0 copy-done.5
  32.6 0.0 copy-start.3
  32.6 0.9 copy-done.3
  33.5 0.0 copy-start.4
  33.5 0.8 copy-done.4
  34.3 5.6 %attend.1 = (bf16[64,256,128]{2,1,0:T(8,128)(2,1)}, bf16[64,256,128]{2,1,0:T(8,128)(2,1)}, bf16[64,2048]{1,0:T(8,128)(2,1)S(1)}) custom-call(bf16[16,64,128]{2,1,0:T(8,128)(2,1)S(1)} %copy-done.3, bf16[4,64,128]{2,1,0:T(8,128)(2,1)S(1)} %copy-done.4, s32[64]{0:T(128)S(1)} %copy-done.5, bf16[64,256,128]{2,1,0:T(8,128)(2,1)S(1)} %bitcast.10, ...), custom_call_target="tpu_custom_call" | custom-call | tf_op jit(solution)/shard_map/attend/pallas_call | solution.py:242
  40.0 0.0 copy-start.2
  40.0 0.7 copy-done.2
  40.7 119.6 %mlp.1 = bf16[128,4096]{1,0:T(8,128)(2,1)} custom-call(bf16[64,2048]{1,0:T(8,128)(2,1)} %copy-done.2, bf16[128,4096]{1,0:T(8,128)(2,1)} %hid_hbm.1, bf16[32,128]{1,0:T(8,128)(2,1)} %bitcast.17, bf16[8,256,4096]{2,1,0:T(8,128)(2,1)} %bitcast.12, bf16[4096,5504]{1,0:T(8,128)(2,1)} %wg.1, bf16[4096,5504]{1,0:T(8,128)(2,1)} %wu.1, bf16[5504,4096]{1,0:T(8,128)(2,1)} %wd.1), custom_call_target="tpu_custom_call" | custom-call | tf_op jit(solution)/shard_map/mlp/pallas_call | solution.py:696
  160.3 2.3 %copy.19 = bf16[128,4096]{1,0:T(8,128)(2,1)} copy(bf16[128,4096]{1,0:T(8,128)(2,1)} %mlp.1) | data formatting | bytes 2097152
Async XLA Ops:
  0.6 31.9 %copy-start = (bf16[64,128,2,128]{3,2,1,0:T(2,128)(2,1)S(1)}, bf16[64,128,2,128]{3,2,1,0:T(2,128)(2,1)}, u32[]{:S(2)}) copy-start(bf16[64,128,2,128]{3,2,1,0:T(2,128)(2,1)} %param.25) | copy-start | bytes 12582916
  0.6 31.9 %copy-start.1 = (bf16[64,128,2,128]{3,2,1,0:T(2,128)(2,1)S(1)}, bf16[64,128,2,128]{3,2,1,0:T(2,128)(2,1)}, u32[]{:S(2)}) copy-start(bf16[64,128,2,128]{3,2,1,0:T(2,128)(2,1)} %param.26) | copy-start | bytes 12582916
  0.7 31.9 %copy-start.5 = (s32[64]{0:T(128)S(1)}, s32[64]{0:T(128)}, u32[]{:S(2)}) copy-start(s32[64]{0:T(128)} %len_ref.1) | copy-start | bytes 772
  32.6 1.0 copy-start.3
  33.5 0.8 copy-start.4
  40.0 0.7 copy-start.2

commit v3 on v2

--- a/solution.py
+++ b/solution.py
@@ -29,8 +29,8 @@
     return jnp.broadcast_to(vec, (128, 128)).T[:, 0:1]
 
 
-KC = 8
-VLIM = 55
+KC = 4
+VLIM = 60
 PAIRS = 10
 
 
@@ -93,13 +93,13 @@
     def send(i):
         return pltpu.make_async_remote_copy(part.at[i, other, :], rbuf.at[i], ss.at[i], rs.at[i], device_id=peer, device_id_type=MESH)
 
-    def product(i):
-        part[i] = jnp.dot(x_s[...], wall[i], preferred_element_type=F32)
-        send(i).start()
-
-    @pl.loop(0, 2)
-    def _(i):
-        product(i)
+    def products(i):
+        for k in range(2):
+            part[i + k] = jnp.dot(x_s[...], wall[i + k], preferred_element_type=F32)
+        for k in range(2):
+            send(i + k).start()
+
+    products(0)
 
     r_h = lax.broadcasted_iota(jnp.int32, (128, 256), 0)
     c_h = lax.broadcasted_iota(jnp.int32, (128, 256), 1)
@@ -120,9 +120,8 @@
                     rows = slice(16 * h, 16 * h + 16)
                     wall[2 + 4 * half + h // 2, to, (h % 2) * 128:(h % 2) * 128 + 128] = jnp.concatenate([d[rows, 0:128], d[rows, 128:256]], axis=0)
 
-        @pl.loop(2 + 4 * half, 6 + 4 * half)
-        def _(i):
-            product(i)
+        products(2 + 4 * half)
+        products(4 + 4 * half)
 
     ins[2].wait()
     ins[3].wait()
@@ -174,7 +173,7 @@
 AROWS = 64 // ACH
 
 
-def attn_kernel(q_ref, kv_ref, len_ref, kc, vc, ko, vo, o_hbm, kb, vb, qs, os, o_ref, isem, osem, obsem):
+def attn_kernel(q_hbm, kv_hbm, len_ref, kc, vc, ko, vo, o_hbm, kb, vb, qs, os, o_ref, q_ref, kv_ref, isem, osem, obsem, qsem):
     def cin(ch, t):
         rows = pl.ds(ch * AROWS, AROWS)
         return pltpu.make_async_copy((kc, vc)[t].at[rows], (kb, vb)[t].at[rows], isem.at[t, ch])
@@ -183,9 +182,14 @@
         rows = pl.ds(ch * AROWS, AROWS)
         return pltpu.make_async_copy((kb, vb)[t].at[rows], (ko, vo)[t].at[rows], osem.at[t, ch])
 
+    ins = [pltpu.make_async_copy(q_hbm, q_ref, qsem.at[0]), pltpu.make_async_copy(kv_hbm, kv_ref, qsem.at[1])]
+    for cp in ins:
+        cp.start()
     for ch in range(ACH):
         for t in range(2):
             cin(ch, t).start()
+    for cp in ins:
+        cp.wait()
     for h in range(16):
         qs[pl.ds(h, 64, stride=16), :] = q_ref[h].astype(F32)
     row16 = lax.broadcasted_iota(jnp.int32, (16, 128), 0)
@@ -242,10 +246,11 @@
     return pl.pallas_call(
         attn_kernel,
         out_shape=(cache, cache, jax.ShapeDtypeStruct((64, 2048), BF16)),
-        in_specs=[VM, VM, SM, ANY, ANY], out_specs=(ANY, ANY, HB),
+        in_specs=[HB, HB, SM, HB, HB], out_specs=(HB, HB, HB),
         scratch_shapes=[pltpu.VMEM((64, 256, 128), BF16), pltpu.VMEM((64, 256, 128), BF16), pltpu.VMEM((1024, 128), F32), pltpu.VMEM((1024, 128), F32), pltpu.VMEM((64, 2048), BF16),
-                        pltpu.SemaphoreType.DMA((2, ACH)), pltpu.SemaphoreType.DMA((2, ACH)), pltpu.SemaphoreType.DMA],
-        compiler_params=pltpu.CompilerParams(vmem_limit_bytes=32 * 2**20),
+                        pltpu.VMEM((16, 64, 128), BF16), pltpu.VMEM((4, 64, 128), BF16),
+                        pltpu.SemaphoreType.DMA((2, ACH)), pltpu.SemaphoreType.DMA((2, ACH)), pltpu.SemaphoreType.DMA, pltpu.SemaphoreType.DMA((2,))],
+        compiler_params=pltpu.CompilerParams(vmem_limit_bytes=60 * 2**20),
         name='attend',
     )(q_rot, kv_new, seq_lens, k_cache, v_cache)
 

time: 163 us -> 161 us (0.988)
  local copies, waits for them, and re-layouts: 4.78 us -> 2.29 us
    pallas_call x1, Pallas kernels: 5.64 us -> 8.42 us  [attn_call(): pl.pallas_call(attn_kernel, out_shape=(cache, cache, jax.ShapeDtypeStruct...]
    unnamed x13 -> x1, local copies, waits for them, and re-layouts: 4.78 us -> 2.29 us
    pallas_call x1, Pallas kernels: 31.9 us -> 29.9 us  [qkv_call(): pl.pallas_call(functools.partial(qkv_kernel, width_full), out_shape=(jax....]
where the time goes in v3:
time: 161 us
  Pallas kernels  158 us (98%)
  local copies, waits for them, and re-layouts  2.29 us (1%)
    pallas_call x1, Pallas kernels, mlp_call(): pl.pallas_call(functools.partial(mlp_kernel, width_full), out_shape=jax.S...  120 us
    pallas_call x1, Pallas kernels, qkv_call(): pl.pallas_call(functools.partial(qkv_kernel, width_full), out_shape=(jax....  29.9 us
    pallas_call x1, Pallas kernels, attn_call(): pl.pallas_call(attn_kernel, out_shape=(cache, cache, jax.ShapeDtypeStruct...  8.42 us

profile of v3, /device:TPU:0, one launch (start us, length us, event | category | flops | bytes accessed | tf_op | source)
XLA Modules:
  0.0 160.8 jit_solution(5347936849734352986)
XLA Ops:
  0.6 29.9 %qkv.1 = (bf16[16,64,128]{2,1,0:T(8,128)(2,1)}, bf16[4,64,128]{2,1,0:T(8,128)(2,1)}) custom-call(bf16[128,4096]{1,0:T(8,128)(2,1)} %hid_hbm.1, bf16[32,128]{1,0:T(8,128)(2,1)} %bitcast.16, f32[64,64]{1,0:T(8,128)} %cos_hbm.1, f32[64,64]{1,0:T(8,128)} %sin_hbm.1, bf16[65536,128]{1,0:T(8,128)(2,1)} %bitcast.11, bf16[8192,128]{1,0:T(8,128)(2,1)} %bitcast.14, ...), custom_call_target="tpu_custom_call" | custom-call | tf_op jit(solution)/shard_map/qkv/pallas_call | solution.py:152
  30.5 8.4 %attend.1 = (bf16[64,256,128]{2,1,0:T(8,128)(2,1)}, bf16[64,256,128]{2,1,0:T(8,128)(2,1)}, bf16[64,2048]{1,0:T(8,128)(2,1)}) custom-call(bf16[16,64,128]{2,1,0:T(8,128)(2,1)} %get-tuple-element.8.q_hbm, bf16[4,64,128]{2,1,0:T(8,128)(2,1)} %get-tuple-element.9.kv_hbm, s32[64]{0:T(128)} %len_ref.1, bf16[64,256,128]{2,1,0:T(8,128)(2,1)} %bitcast.12, ...), custom_call_target="tpu_custom_call" | custom-call | tf_op jit(solution)/shard_map/attend/pallas_call | solution.py:246
  39.0 119.6 %mlp.1 = bf16[128,4096]{1,0:T(8,128)(2,1)} custom-call(bf16[64,2048]{1,0:T(8,128)(2,1)} %get-tuple-element.10.o_hbm, bf16[128,4096]{1,0:T(8,128)(2,1)} %hid_hbm.1, bf16[32,128]{1,0:T(8,128)(2,1)} %bitcast.17, bf16[8,256,4096]{2,1,0:T(8,128)(2,1)} %bitcast.10, bf16[4096,5504]{1,0:T(8,128)(2,1)} %wg.1, bf16[4096,5504]{1,0:T(8,128)(2,1)} %wu.1, ...), custom_call_target="tpu_custom_call" | custom-call | tf_op jit(solution)/shard_map/mlp/pallas_call | solution.py:701
  158.5 2.3 %copy.19 = bf16[128,4096]{1,0:T(8,128)(2,1)} copy(bf16[128,4096]{1,0:T(8,128)(2,1)} %mlp.1) | data formatting | bytes 2097152

commit v4 on v3

--- a/solution.py
+++ b/solution.py
@@ -169,7 +169,7 @@
     )(hidden, gain, cos, sin, wq, wk, wv)
 
 
-ACH = 4
+ACH = 2
 AROWS = 64 // ACH
 
 
@@ -261,13 +261,13 @@
 ND = 8
 NR = 4
 RB = 128 // NR
-LEAD = 5
+LEAD = 6
 LAG = 2
-DLAG = 5
+DLAG = 6
 
 
 def mlp_kernel(width_full, o_hbm, hid_hbm, gain_hbm, wo, wg, wu, wd, out,
-               o_ref, hid, gain, insem, wbuf, dbuf, oall, acc, dd, xs, xr, hq, oq, x2, gown, gsnd, grcv, mall, st,
+               o_ref, hid, gain, insem, outv, outsem, wbuf, dbuf, oall, acc, dd, xs, xr, hq, oq, x2, gown, gsnd, grcv, mall, st,
                wsem, dsem, osem, d2d, xx, agc, agx, fwd, stsem, gs, gr, ms, mr):
     dp, dm, tp = me()
     x = tp // 2
@@ -669,6 +669,18 @@
         d2d_cp(1, 1, r).start()
     for r in (2, 3):
         chip_sum(1, r)
+
+    def put(r):
+        return pltpu.make_async_copy(outv.at[rows_of(r)], out.at[rows_of(r)], outsem.at[r])
+
+    def emit(r):
+        arrived(1, r, oq)
+        for q in range(4):
+            outv[rows_of(r), 1024 * q:1024 * q + 1024] = oq[q, blk(r), :]
+        put(r).start()
+
+    emit(0)
+    emit(1)
     for r in (2, 3):
         mlp = total(1, r)
         oq[tp, blk(r)] = (hq[tp, blk(r)].astype(F32) + mlp.astype(F32)).astype(BF16)
@@ -688,12 +700,11 @@
             g_cp(b, ch).wait_send()
             m_cp(b, ch).wait_send()
 
-    for r in range(NR):
-        arrived(1, r, oq)
-        for q in range(4):
-            out[rows_of(r), 1024 * q:1024 * q + 1024] = oq[q, blk(r), :]
+    emit(2)
+    emit(3)
     for r in range(NR):
         drained(1, r, oq)
+        put(r).wait()
 
 
 def mlp_call(o, hidden, gain, wo, wg, wu, wd, width_full):
@@ -701,9 +712,10 @@
     return pl.pallas_call(
         functools.partial(mlp_kernel, width_full),
         out_shape=jax.ShapeDtypeStruct((128, 4096), BF16),
-        in_specs=[HB] * 7, out_specs=VM,
+        in_specs=[HB] * 7, out_specs=HB,
         scratch_shapes=[
             pltpu.VMEM((64, 2048), BF16), pltpu.VMEM((128, 4096), BF16), pltpu.VMEM((32, 128), BF16), dma((3,)),
+            pltpu.VMEM((128, 4096), BF16), dma((NR,)),
             pltpu.VMEM((NB, 2, 4096, C), BF16),
             pltpu.VMEM((ND, C, 4096), BF16),
             pltpu.VMEM((64, 2048), BF16),
@@ -728,6 +740,30 @@
     )(o, hidden, gain, wo, wg, wu, wd)
 
 
+def copy_kernel(src, dst, buf, isem, osem):
+    def part(a, b, sem, i):
+        rows = pl.ds(32 * i, 32)
+        return pltpu.make_async_copy(a.at[rows], b.at[rows], sem.at[i])
+
+    for i in range(4):
+        part(src, buf, isem, i).start()
+    for i in range(4):
+        part(src, buf, isem, i).wait()
+        part(buf, dst, osem, i).start()
+    for i in range(4):
+        part(buf, dst, osem, i).wait()
+
+
+def copy_call(h):
+    return pl.pallas_call(
+        copy_kernel,
+        out_shape=jax.ShapeDtypeStruct(h.shape, h.dtype),
+        in_specs=[HB], out_specs=HB,
+        scratch_shapes=[pltpu.VMEM((128, 4096), BF16), pltpu.SemaphoreType.DMA((4,)), pltpu.SemaphoreType.DMA((4,))],
+        name='copy_out',
+    )(h)
+
+
 def solution(mesh):
     width_shards = mesh.shape['dm']
     row_spec = P('dp', 'dm')
@@ -742,6 +778,7 @@
         q_rot, kv_new = qkv_call(hidden, norm_attn.reshape(-1, 128), rope_cos, rope_sin, w_q.reshape(-1, 128), w_k.reshape(-1, 128), w_v.reshape(-1, 128), width_full)
         k_out, v_out, o = attn_call(q_rot, kv_new, seq_lens, k_cache.reshape(64, 256, 128), v_cache.reshape(64, 256, 128))
         h_out = mlp_call(o, hidden, norm_mlp.reshape(-1, 128), w_o.reshape(8, 256, -1), w_gate, w_up, w_down, width_full)
+        h_out = copy_call(h_out)
         return h_out, k_out.reshape(k_cache.shape), v_out.reshape(v_cache.shape)
 
     return jax.shard_map(local_layer, mesh=mesh, in_specs=in_specs, out_specs=out_specs, check_vma=False)

time: 161 us -> 159 us (0.988)
  local copies, waits for them, and re-layouts: 2.29 us -> 0 us
    unnamed x1 -> x0, local copies, waits for them, and re-layouts: 2.29 us -> none
    pallas_call x0 -> x1, Pallas kernels: none -> 1.98 us  [copy_call(): pl.pallas_call(copy_kernel, out_shape=jax.ShapeDtypeStruct(h.shape, h.dty...]
where the time goes in v4:
time: 159 us
  Pallas kernels  158 us (99%)
    pallas_call x1, Pallas kernels, mlp_call(): pl.pallas_call(functools.partial(mlp_kernel, width_full), out_shape=jax.S...  118 us
    pallas_call x1, Pallas kernels, qkv_call(): pl.pallas_call(functools.partial(qkv_kernel, width_full), out_shape=(jax....  29.9 us
    pallas_call x1, Pallas kernels, attn_call(): pl.pallas_call(attn_kernel, out_shape=(cache, cache, jax.ShapeDtypeStruct...  7.93 us

profile of v4, /device:TPU:0, one launch (start us, length us, event | category | flops | bytes accessed | tf_op | source)
XLA Modules:
  0.0 158.8 jit_solution(10827771807237487745)
XLA Ops:
  0.6 29.9 %qkv.1 = (bf16[16,64,128]{2,1,0:T(8,128)(2,1)}, bf16[4,64,128]{2,1,0:T(8,128)(2,1)}) custom-call(bf16[128,4096]{1,0:T(8,128)(2,1)} %hid_hbm.1, bf16[32,128]{1,0:T(8,128)(2,1)} %bitcast.16, f32[64,64]{1,0:T(8,128)} %cos_hbm.1, f32[64,64]{1,0:T(8,128)} %sin_hbm.1, bf16[65536,128]{1,0:T(8,128)(2,1)} %bitcast.11, bf16[8192,128]{1,0:T(8,128)(2,1)} %bitcast.14, ...), custom_call_target="tpu_custom_call" | custom-call | tf_op jit(solution)/shard_map/qkv/pallas_call | solution.py:152
  30.5 7.9 %attend.1 = (bf16[64,256,128]{2,1,0:T(8,128)(2,1)}, bf16[64,256,128]{2,1,0:T(8,128)(2,1)}, bf16[64,2048]{1,0:T(8,128)(2,1)}) custom-call(bf16[16,64,128]{2,1,0:T(8,128)(2,1)} %get-tuple-element.8.q_hbm, bf16[4,64,128]{2,1,0:T(8,128)(2,1)} %get-tuple-element.9.kv_hbm, s32[64]{0:T(128)} %len_ref.1, bf16[64,256,128]{2,1,0:T(8,128)(2,1)} %bitcast.12, ...), custom_call_target="tpu_custom_call" | custom-call | tf_op jit(solution)/shard_map/attend/pallas_call | solution.py:246
  38.5 118.2 %mlp.1.src = bf16[128,4096]{1,0:T(8,128)(2,1)} custom-call(bf16[64,2048]{1,0:T(8,128)(2,1)} %get-tuple-element.10.o_hbm, bf16[128,4096]{1,0:T(8,128)(2,1)} %hid_hbm.1, bf16[32,128]{1,0:T(8,128)(2,1)} %bitcast.17, bf16[8,256,4096]{2,1,0:T(8,128)(2,1)} %bitcast.10, bf16[4096,5504]{1,0:T(8,128)(2,1)} %wg.1, bf16[4096,5504]{1,0:T(8,128)(2,1)} %wu.1, ...), custom_call_target="tpu_custom_call" | custom-call | tf_op jit(solution)/shard_map/mlp/pallas_call | solution.py:712
  156.7 2.0 %copy_out.1 = bf16[128,4096]{1,0:T(8,128)(2,1)} custom-call(bf16[128,4096]{1,0:T(8,128)(2,1)} %mlp.1.src), custom_call_target="tpu_custom_call" | custom-call | tf_op jit(solution)/shard_map/copy_out/pallas_call | solution.py:758
